TPU v7x, 256 devices: a whole 4x4x8 slice. The times are simulated.
256 devices in a mesh: view: 4 (over x_hi, core), pencil: 64 (over x_lo, y, z).
Axes of the slice: x: 4 (x_hi: 2, x_lo: 2; x = x_hi * 2 + x_lo), y: 4, z: 8, core: 2. Of those that a mesh axis runs over, the one named last changes fastest.
Arguments:
- recorded: float32 [4, 256, 256, 256], P('view', 'pencil'), may hold values from 0.5 to 4
- spectral_weight: float32 [4, 256, 256, 256], P('view', None, 'pencil'), may hold values from 0.05 to 1
- psf_taps: float32 [4, 3, 9], replicated, may hold values from 0.1 to 1
Outputs:
- joined_volume: float32 [256, 256, 256], P('pencil', 'view')
- estimate: float32 [256, 256, 256], P('pencil', 'view')
All inputs are finite; a program needn't handle non-finite values.
Results may differ from a plain program's by a relative error of at most 0.00029.
Values sent between devices are 32-bit elements; how exact they have to be, the bound alone decides.
A program may use at most 64 MiB of HBM per device.

v0:
```python
import functools

import jax
import jax.numpy as jnp
import numpy as np
from jax import lax
from jax.experimental import pallas as pl
from jax.experimental.pallas import tpu as pltpu
from jax.sharding import PartitionSpec as P

ITERS = 2
MESH_ID = pl.DeviceIdType.MESH
F32 = jnp.float32
BF16 = jnp.bfloat16
SIDES = [(dv, dp) for dp in (-1, 1, 0) for dv in (0, -1, 1) if (dv, dp) != (0, 0)]
SLOT = {side: k for k, side in enumerate(SIDES)}


def halves(value):
    high = value.astype(BF16)
    return high, (value - high.astype(F32)).astype(BF16)


def dot(left, right):
    return jnp.dot(left, right, preferred_element_type=F32)


def dot3(left, right_high, right_low):
    high, low = halves(left)
    return dot(high, right_high) + (dot(high, right_low) + dot(low, right_high))


def rl_kernel(views, pencils, taps, joined, stacked, out, est, zed, mid, spread, acc, rz, rs,
              th, tl, ah, al, send_sem, recv_sem):
    depth, rows, width = joined.shape
    frame = rows + 16
    v0, p0 = lax.axis_index("view"), lax.axis_index("pencil")

    def exists(side):
        v, p = v0 + side[0], p0 + side[1]
        return (v >= 0) & (v < views) & (p >= 0) & (p < pencils)

    def back(side):
        return (-side[0], -side[1])

    est[...] = jnp.zeros_like(est)
    mid[...] = jnp.zeros_like(mid)
    rz[...] = jnp.zeros_like(rz)
    rs[...] = jnp.zeros_like(rs)

    barrier = pltpu.get_barrier_semaphore()
    for side in SIDES:
        @pl.when(exists(side))
        def _(side=side):
            pl.semaphore_signal(barrier, inc=1, device_id=(v0 + side[0], p0 + side[1]), device_id_type=MESH_ID)

    planes_of = {-1: pl.ds(0, depth), 0: pl.ds(depth, depth), 1: pl.ds(2 * depth, depth)}

    def est_copy(side):
        dv, dp = side
        src_rows = {0: pl.ds(8, rows), 1: pl.ds(rows, 8), -1: pl.ds(8, 8)}[dv]
        dst_rows = {0: pl.ds(8, rows), 1: pl.ds(0, 8), -1: pl.ds(rows + 8, 8)}[dv]
        return pltpu.make_async_remote_copy(
            src_ref=est.at[planes_of[0], :, src_rows, :],
            dst_ref=est.at[planes_of[-dp], :, dst_rows, :],
            send_sem=send_sem.at[0, SLOT[side]],
            recv_sem=recv_sem.at[0, SLOT[back(side)]],
            device_id=(v0 + dv, p0 + dp),
            device_id_type=MESH_ID,
        )

    def acc_copy(side):
        dv, dp = side
        src_rows = {0: pl.ds(8, rows), 1: pl.ds(rows + 8, 8), -1: pl.ds(0, 8)}[dv]
        slot = SLOT[back(side)]
        landing = rz.at[0 if dp == 1 else 1] if dv == 0 else rs.at[slot]
        return pltpu.make_async_remote_copy(
            src_ref=acc.at[planes_of[dp], :, src_rows, :],
            dst_ref=landing,
            send_sem=send_sem.at[1, SLOT[side]],
            recv_sem=recv_sem.at[1, slot],
            device_id=(v0 + dv, p0 + dp),
            device_id_type=MESH_ID,
        )

    def each(sides, action):
        for side in sides:
            @pl.when(exists(side))
            def _(side=side):
                action(side)

    for h in range(2):
        s = joined[:, :, h * 128:(h + 1) * 128]
        est[pl.ds(depth, depth), h, pl.ds(8, rows), :] = 0.1 + (
            jnp.maximum(s, 0.0) + jnp.log1p(jnp.exp(-jnp.abs(s))))

    expected = sum(exists(side).astype(jnp.int32) for side in SIDES)
    pl.semaphore_wait(barrier, expected)
    each(SIDES, lambda side: est_copy(side).start())

    def band(v, carry):
        at = (lax.broadcasted_iota(jnp.int32, (width, width), 0)
              - lax.broadcasted_iota(jnp.int32, (width, width), 1))
        table, turned = jnp.zeros((width, width), F32), jnp.zeros((width, width), F32)
        for t in range(9):
            tap = taps[v, 2, t]
            table = jnp.where(at == t - 4, tap, table)
            turned = jnp.where(at == 4 - t, tap, turned)
        th[v], tl[v] = halves(table)
        ah[v], al[v] = halves(turned)
        return carry

    lax.fori_loop(0, views, band, 0)

    def view_step(v, carry):
        for z in range(depth):
            total = taps[v, 0, 0] * est[z]
            for t in range(1, 9):
                total = total + taps[v, 0, t] * est[z + t]
            zed[z] = total
        sides = []
        for h in range(2):
            planes = []
            for z in range(depth):
                total = taps[v, 1, 0] * zed[z, h, pl.ds(4, rows), :]
                for t in range(1, 9):
                    total = total + taps[v, 1, t] * zed[z, h, pl.ds(4 + t, rows), :]
                planes.append(total)
            sides.append(jnp.concatenate(planes, axis=0))
        blurred = dot3(jnp.concatenate(sides, axis=1), th[v], tl[v])
        ratio = stacked[v].reshape(depth * rows, width) / blurred
        turned = dot3(ratio, ah[v], al[v])
        for z in range(depth):
            for h in range(2):
                mid[z, h, pl.ds(16, rows), :] = turned[z * rows:(z + 1) * rows, h * 128:(h + 1) * 128]
        for z in range(depth):
            for h in range(2):
                total = taps[v, 1, 8] * mid[z, h, pl.ds(4, frame), :]
                for t in range(1, 9):
                    total = total + taps[v, 1, 8 - t] * mid[z, h, pl.ds(4 + t, frame), :]
                spread[v, z, h] = total
        return carry

    def gather_planes(planes):
        for zo in planes:
            total = None
            for v in range(views):
                for zs in range(depth):
                    if 0 <= zo - zs <= 8:
                        term = taps[v, 0, zo - zs] * spread[v, zs]
                        total = term if total is None else total + term
            acc[zo] = total

    def iteration(step, carry):
        each(SIDES, est_wait)
        lax.fori_loop(0, views, view_step, 0)
        gather_planes(list(range(0, depth)) + list(range(2 * depth, 3 * depth)))
        each([s for s in SIDES if s[1] != 0], lambda side: acc_copy(side).start())
        gather_planes(range(depth, 2 * depth))
        each([s for s in SIDES if s[1] == 0], lambda side: acc_copy(side).start())
        each(SIDES, lambda side: est_copy(side).wait_send())
        each(SIDES, acc_wait)
        for z in range(depth):
            for h in range(2):
                total = acc[depth + z, h, pl.ds(8, rows), :] + (rz[0, z, h] + rz[1, z, h])
                low = rs[SLOT[(-1, 0)], z, h] + (rs[SLOT[(-1, -1)], z, h] + rs[SLOT[(-1, 1)], z, h])
                high = rs[SLOT[(1, 0)], z, h] + (rs[SLOT[(1, -1)], z, h] + rs[SLOT[(1, 1)], z, h])
                total = jnp.concatenate(
                    [total[:8] + low, total[8:rows - 8], total[rows - 8:] + high], axis=0)
                fresh = est[depth + z, h, pl.ds(8, rows), :] * (total * (1.0 / views))
                est[depth + z, h, pl.ds(8, rows), :] = fresh
        each(SIDES, lambda side: acc_copy(side).wait_send())

        @pl.when(step < ITERS - 1)
        def _():
            each(SIDES, lambda side: est_copy(side).start())
        return carry

    def est_wait(side):
        dv, dp = side
        dst_rows = {0: pl.ds(8, rows), -1: pl.ds(0, 8), 1: pl.ds(rows + 8, 8)}[dv]
        landing = est.at[planes_of[dp], :, dst_rows, :]
        pltpu.make_async_remote_copy(
            src_ref=landing, dst_ref=landing, send_sem=send_sem.at[0, SLOT[side]],
            recv_sem=recv_sem.at[0, SLOT[side]], device_id=(v0 + dv, p0 + dp),
            device_id_type=MESH_ID).wait_recv()

    def acc_wait(side):
        dv, dp = side
        landing = rz.at[0 if dp == -1 else 1] if dv == 0 else rs.at[SLOT[side]]
        pltpu.make_async_remote_copy(
            src_ref=landing, dst_ref=landing, send_sem=send_sem.at[1, SLOT[side]],
            recv_sem=recv_sem.at[1, SLOT[side]], device_id=(v0 + dv, p0 + dp),
            device_id_type=MESH_ID).wait_recv()

    lax.fori_loop(0, ITERS, iteration, 0)
    for h in range(2):
        out[:, :, h * 128:(h + 1) * 128] = est[pl.ds(depth, depth), h, pl.ds(8, rows), :]


def richardson_lucy(joined, stacked, kernels):
    views, pencils = stacked.shape[0], lax.axis_size("pencil")
    depth, rows, width = joined.shape
    frame = rows + 16
    vmem = pl.BlockSpec(memory_space=pltpu.VMEM)
    return pl.pallas_call(
        functools.partial(rl_kernel, views, pencils),
        name="deconvolve",
        out_shape=jax.ShapeDtypeStruct(joined.shape, F32),
        in_specs=[pl.BlockSpec(memory_space=pltpu.SMEM), vmem, vmem],
        out_specs=vmem,
        scratch_shapes=[
            pltpu.VMEM((3 * depth, 2, frame, 128), F32),
            pltpu.VMEM((depth, 2, frame, 128), F32),
            pltpu.VMEM((depth, 2, frame + 16, 128), F32),
            pltpu.VMEM((views, depth, 2, frame, 128), F32),
            pltpu.VMEM((3 * depth, 2, frame, 128), F32),
            pltpu.VMEM((2, depth, 2, rows, 128), F32),
            pltpu.VMEM((8, depth, 2, 8, 128), F32),
            pltpu.VMEM((views, width, width), BF16),
            pltpu.VMEM((views, width, width), BF16),
            pltpu.VMEM((views, width, width), BF16),
            pltpu.VMEM((views, width, width), BF16),
            pltpu.SemaphoreType.DMA((2, 8)),
            pltpu.SemaphoreType.DMA((2, 8)),
        ],
        compiler_params=pltpu.CompilerParams(collective_id=1, has_side_effects=True,
                                             vmem_limit_bytes=24 * 1024 * 1024),
    )(kernels, joined, stacked)


def two_terms(table):
    high = table.astype(jnp.bfloat16)
    low = (table - high.astype(np.float64)).astype(jnp.bfloat16)
    return [high, low]


def transform_tables(n, nx):
    at = np.arange(n)
    phase = 2.0 * np.pi * (at[:, None] * at[None, :] % n) / n
    cosine, sine = np.cos(phase), np.sin(phase)
    q = n // 4
    rows = np.concatenate([cosine.reshape(4, q, n), sine.reshape(4, q, n)], axis=1)

    x, c = np.arange(nx)[:, None], np.arange(nx // 2)[None, :]
    wave = 2.0 * np.pi * (x * c % nx) / nx
    sign = np.where(x % 2 == 0, 1.0, -1.0)
    columns = np.concatenate([np.cos(wave), np.where(c == 0, sign, -np.sin(wave))], axis=1)
    scale = 1.0 / (float(n) * n * nx)
    back_re = np.where(c == 0, 1.0, 2.0 * np.cos(wave)).T
    back_im = np.where(c == 0, sign, -2.0 * np.sin(wave)).T
    columns_back = np.concatenate([back_re, back_im], axis=0) * scale

    index = np.arange(2 * n)
    part, depth = index % 8 // 4, index // 8 * 4 + index % 4
    c_z, s_z = cosine[:, depth], sine[:, depth]
    depth_table = np.concatenate(
        [np.where(part == 0, c_z, s_z), np.where(part == 0, -s_z, c_z)], axis=0)

    m = np.arange(n // 2)
    back = []
    for core in range(2):
        ky = m // 2 * 4 + 2 * core + m % 2
        back.append(np.concatenate([cosine[:, ky], sine[:, ky]], axis=1))
    return [t for table in (rows, columns, depth_table, np.stack(back), columns_back)
            for t in two_terms(table)]


def right3(high, low, right):
    r_high, r_low = halves(right)
    return dot(high, r_high) + (dot(high, r_low) + dot(low, r_high))


def left3(left, high, low):
    l_high, l_low = halves(left)
    return dot(l_high, high) + (dot(l_high, low) + dot(l_low, high))


def reversal(n):
    total = lax.broadcasted_iota(jnp.int32, (n, n), 0) + lax.broadcasted_iota(jnp.int32, (n, n), 1)
    return jnp.where((total == 0) | (total == n), 1.0, 0.0).astype(BF16)


def moved_right(value, table):
    high, low = halves(value)
    return dot(high, table) + dot(low, table)


def moved_left(table, value):
    high, low = halves(value)
    return dot(table, high) + dot(table, low)


def join_kernel(pencils, slab, weight, csh, csl, dxh, dxl, mh, ml, cyh, cyl, dih, dil, out,
                xh, xl, msg, got, wsend, wgot, we, wm, mth, mtl, g, gr, gm, fr, pj, r1, r2,
                ssem, rsem, lsem):
    n = 4 * pencils
    q = n // 4
    half = pencils // 2
    v, p = lax.axis_index("view"), lax.axis_index("pencil")
    core = lax.rem(v, 2)
    mate = v + 1 - 2 * core
    far = lax.rem(v + 2, 4)
    mirror = pencils - 1 - p
    mirror0 = lax.rem(pencils - p, pencils)
    own_mirror = (p == 0) | (p == half)

    barrier = pltpu.get_barrier_semaphore()

    def greet(i, carry):
        pl.semaphore_signal(barrier, inc=1, device_id=(v, lax.rem(p + i, pencils)), device_id_type=MESH_ID)
        return carry

    lax.fori_loop(1, pencils, greet, 0)
    pl.semaphore_signal(barrier, inc=1, device_id=(mate, p), device_id_type=MESH_ID)
    pl.semaphore_signal(barrier, inc=1, device_id=(far, p), device_id_type=MESH_ID)

    def remote(src, dst, k, device):
        return pltpu.make_async_remote_copy(
            src_ref=src, dst_ref=dst, send_sem=ssem.at[k], recv_sem=rsem.at[k],
            device_id=device, device_id_type=MESH_ID)

    lane0 = lax.broadcasted_iota(jnp.int32, (n, 128), 1) == 0

    for j in range(4):
        receiver = mirror0 if j == 0 else mirror
        pick = lane0 & (receiver < half)
        wsend[j] = jnp.where(pick, weight[0, j], weight[1, j])

    pl.semaphore_wait(barrier, pencils + 1)
    w_rest = remote(wsend.at[pl.ds(1, 3)], wgot.at[pl.ds(1, 3)], 1, (v, mirror))
    w_first = remote(wsend.at[0], wgot.at[0], 2, (v, mirror0))
    w_local = pltpu.make_async_copy(wsend.at[0], wgot.at[0], lsem.at[0])
    w_rest.start()

    @pl.when(jnp.logical_not(own_mirror))
    def _():
        w_first.start()

    @pl.when(own_mirror)
    def _():
        w_local.start()

    for z in range(4):
        xh[z], xl[z] = halves(left3(slab[z], dxh[...], dxl[...]))

    lane_q = lax.broadcasted_iota(jnp.int32, (q, 128), 1) == 0
    row_q = lax.broadcasted_iota(jnp.int32, (q, 128), 0)

    def send_chunk(i, carry):
        peer = carry + i
        at = pl.multiple_of(peer * 32, 32)

        @pl.when(peer != p)
        def _():
            remote(msg.at[pl.ds(at, 32)], got.at[p], 0, (v, peer)).start()
        return carry

    for b in range(4):
        for z in range(4):
            both = (dot(csh[b], xh[z]) + (dot(csh[b], xl[z]) + dot(csl[b], xh[z])))
            c_re, c_im = both[:q, :128], both[:q, 128:]
            s_re, s_im = both[q:, :128], both[q:, 128:]
            re, im = c_re + s_im, c_im - s_re
            re0 = c_re if b < 2 else c_im
            im0 = -s_re if b < 2 else -s_im
            if b == 0:
                im0 = jnp.where(row_q == 0, c_im, im0)
            if b == 2:
                im0 = jnp.where(row_q == 0, c_re, im0)
            msg[pl.ds(b * q * 8 + z, q, stride=8), :] = jnp.where(lane_q, re0, re)
            msg[pl.ds(b * q * 8 + 4 + z, q, stride=8), :] = jnp.where(lane_q, im0, im)
        lax.fori_loop(0, pencils // 4, send_chunk, b * (pencils // 4))

    own = pltpu.make_async_copy(msg.at[pl.ds(pl.multiple_of(p * 32, 32), 32)], got.at[p], lsem.at[1])
    own.start()

    mth[...] = mh[...].astype(F32).T.astype(BF16)
    mtl[...] = ml[...].astype(F32).T.astype(BF16)
    w_rest.wait_recv()

    @pl.when(jnp.logical_not(own_mirror))
    def _():
        w_first.wait()

    @pl.when(own_mirror)
    def _():
        w_local.wait()

    turn_z, turn_x = reversal(n), reversal(128)
    for j in range(4):
        mine = jnp.where(lane0 & (p >= half), weight[1, j], weight[0, j])
        turned = moved_left(turn_z, moved_right(wgot[(4 - j) % 4], turn_x))
        we[j] = 0.5 * (mine + turned)

    @pl.when(own_mirror)
    def _():
        first = (lax.broadcasted_iota(jnp.int32, (n, 128), 0) * 0 + p) == 0
        other = jnp.where(first, weight[1, 0], weight[0, 0])
        other = 0.5 * (other + moved_left(turn_z, other))
        main = we[0]
        we[0] = jnp.where(lane0, 0.5 * (main + other), main)
        wm[...] = jnp.where(lane0, 0.5 * (main - other), 0.0)

    own.wait()
    remote(got.at[pl.ds(0, pencils - 1)], got.at[pl.ds(0, pencils - 1)], 0, (v, mirror)).wait_recv()

    def tile_rows(j):
        return got[:, 8 * j:8 * j + 8, :].reshape(2 * n, 128)

    for pair in range(2):
        f = right3(mh[...], ml[...], jnp.concatenate([tile_rows(2 * pair), tile_rows(2 * pair + 1)], axis=1))
        for k in range(2):
            j = 2 * pair + k
            for part in range(2):
                g[j, part * n:(part + 1) * n, :] = (
                    f[part * n:(part + 1) * n, 128 * k:128 * k + 128] * we[j])

    @pl.when(own_mirror)
    def _():
        imag = lax.rem(lax.broadcasted_iota(jnp.int32, (2 * n, 128), 0), 8) >= 4
        rows = tile_rows(0)
        f = right3(mh[...], ml[...], jnp.where(imag, -rows, rows))
        for part in range(2):
            g[0, part * n:(part + 1) * n, :] = (
                g[0, part * n:(part + 1) * n, :] + f[part * n:(part + 1) * n, :] * wm[...])

    pair_sum = remote(g.at[pl.ds(2 - 2 * core, 2)], gr, 3, (mate, p))
    pair_sum.start()
    pair_sum.wait_recv()
    f = right3(mth[...], mtl[...], jnp.concatenate(
        [g[2 * core] + gr[0], g[2 * core + 1] + gr[1]], axis=1))
    gm[:, 0:8, :] = f[:, :128].reshape(pencils, 8, 128)
    gm[:, 8:16, :] = f[:, 128:].reshape(pencils, 8, 128)

    def here(peer):
        return fr.at[pl.ds(pl.multiple_of(peer * 16, 16), 16)]

    def send_back(i, carry):
        peer = lax.rem(p + i, pencils)
        remote(gm.at[peer], here(p), 4, (v, peer)).start()
        return carry

    lax.fori_loop(1, pencils, send_back, 0)
    own_back = pltpu.make_async_copy(gm.at[p], here(p), lsem.at[2])
    own_back.start()
    own_back.wait()
    most = fr.at[pl.ds(0, 16 * (pencils - 1))]
    remote(most, most, 4, (v, mirror)).wait_recv()

    m = lax.broadcasted_iota(jnp.int32, (n // 2, 128), 0)
    ky = m // 2 * 4 + 2 * core + lax.rem(m, 2)
    lane_m = lax.broadcasted_iota(jnp.int32, (n // 2, 128), 1) == 0
    low, high = (ky > 0) & (ky < n // 2), ky > n // 2
    for z in range(4):
        re = fr[pl.ds(z, n // 2, stride=8), :]
        im = fr[pl.ds(4 + z, n // 2, stride=8), :]
        zero = jnp.zeros_like(re)
        v1 = jnp.where(low, 2.0 * re, jnp.where(ky == 0, re, jnp.where(ky == n // 2, im, zero)))
        v2 = jnp.where(high, 2.0 * re, jnp.where(ky == 0, im, jnp.where(ky == n // 2, re, zero)))
        b1 = jnp.where(low, -2.0 * im, zero)
        b2 = jnp.where(high, -2.0 * im, zero)
        top = jnp.concatenate([jnp.where(lane_m, v1, re), jnp.where(lane_m, v2, im)], axis=1)
        bottom = jnp.concatenate([jnp.where(lane_m, b1, -im), jnp.where(lane_m, b2, re)], axis=1)
        u = right3(cyh[core], cyl[core], jnp.concatenate([top, bottom], axis=0))
        rows = left3(u, dih[...], dil[...])
        for quarter in range(4):
            pj[quarter // 2, quarter % 2, z] = rows[quarter * q:(quarter + 1) * q]

    near = remote(pj.at[:, 1 - core], r1, 5, (mate, p))
    near.start()
    near.wait_recv()
    away = lax.rem(v // 2 + 1, 2)
    kept = v // 2
    r1[...] = r1[...] + pj[:, core]
    long = remote(r1.at[away], r2, 6, (far, p))
    long.start()
    long.wait_recv()
    out[...] = r1[kept] + r2[...]

    w_rest.wait_send()
    sent = msg.at[pl.ds(0, 32 * (pencils - 1))]
    remote(sent, sent, 0, (v, mirror)).wait_send()
    pair_sum.wait_send()
    sent_back = gm.at[pl.ds(0, pencils - 1)]
    remote(sent_back, sent_back, 4, (v, mirror)).wait_send()
    near.wait_send()
    long.wait_send()


def spectral_join(slab, weight):
    pencils = lax.axis_size("pencil")
    n, nx = 4 * pencils, slab.shape[-1]
    q = n // 4
    vmem = pl.BlockSpec(memory_space=pltpu.VMEM)
    tables = [jnp.asarray(t) for t in transform_tables(n, nx)]
    return pl.pallas_call(
        functools.partial(join_kernel, pencils),
        name="join",
        out_shape=jax.ShapeDtypeStruct((4, q, nx), F32),
        in_specs=[vmem] * (2 + len(tables)),
        out_specs=vmem,
        scratch_shapes=[
            pltpu.VMEM((4, n, nx), BF16),
            pltpu.VMEM((4, n, nx), BF16),
            pltpu.VMEM((8 * n, 128), F32),
            pltpu.VMEM((pencils, 32, 128), F32),
            pltpu.VMEM((4, n, 128), F32),
            pltpu.VMEM((4, n, 128), F32),
            pltpu.VMEM((4, n, 128), F32),
            pltpu.VMEM((n, 128), F32),
            pltpu.VMEM((2 * n, 2 * n), BF16),
            pltpu.VMEM((2 * n, 2 * n), BF16),
            pltpu.VMEM((4, 2 * n, 128), F32),
            pltpu.VMEM((2, 2 * n, 128), F32),
            pltpu.VMEM((pencils, 16, 128), F32),
            pltpu.VMEM((pencils * 16, 128), F32),
            pltpu.VMEM((2, 2, 4, q, nx), F32),
            pltpu.VMEM((2, 4, q, nx), F32),
            pltpu.VMEM((4, q, nx), F32),
            pltpu.SemaphoreType.DMA((7,)),
            pltpu.SemaphoreType.DMA((7,)),
            pltpu.SemaphoreType.DMA((3,)),
        ],
        compiler_params=pltpu.CompilerParams(collective_id=2, has_side_effects=True,
                                             vmem_limit_bytes=40 * 1024 * 1024),
    )(slab, weight, *tables)


def weight_halves(block):
    n, chunk, nx = block.shape
    return jnp.transpose(block.reshape(n, chunk, 2, nx // 2), (2, 1, 0, 3))


def body(recorded, spectral_weight, psf_taps):
    kernels = psf_taps / jnp.sum(psf_taps, axis=-1, keepdims=True)
    stacked = lax.all_to_all(recorded, "view", split_axis=2, concat_axis=0, tiled=True)
    joined = spectral_join(recorded[0], weight_halves(spectral_weight[0]))
    return (joined, richardson_lucy(joined, stacked, kernels))


def solution(mesh):
    return jax.shard_map(
        body,
        mesh=mesh,
        in_specs=(P("view", "pencil", None, None), P("view", None, "pencil", None), P()),
        out_specs=(P("pencil", "view", None), P("pencil", "view", None)),
        check_vma=False,
    )
```

profile of v0, /device:TPU:3, one launch (start us, length us, event | category | flops | bytes accessed | tf_op | source)
XLA Modules:
  0.0 166.3 jit_solution(4789676632317836504)
XLA Ops:
  0.6 2.9 %copy.24 = f32[1,4,256,256]{3,1,0,2:T(4,128)} copy(f32[1,4,256,256]{3,2,1,0:T(8,128)} %param.13) | data formatting | bytes 2097152 | tf_op args[0]
  3.5 0.0 copy-start.11
  3.5 5.0 %all-to-all-start = ((f32[1,4,256,256]{3,1,0,2:T(4,128)}), f32[1,4,256,256]{3,1,0,2:T(4,128)}, u32[]{:S(2)}, u32[]{:S(2)}) async-start(f32[1,4,256,256]{3,1,0,2:T(4,128)} %copy.24), calls=%async_computation | async-start | bytes 2097152 | tf_op jit(solution)/shard_map/all_to_all | solution.py:537
  8.5 0.0 copy-done.11
  8.5 0.0 copy-start.12
  8.6 0.0 copy-start.7
  8.6 1.4 copy.20
  9.9 0.0 copy-start
  9.9 0.0 copy-start.1
  9.9 0.0 copy-start.2
  9.9 1.7 %copy.21 = f32[256,4,2,128]{3,0,1,2:T(8,128)S(1)} copy(f32[256,4,2,128]{0,3,2,1:T(8,128)} %bitcast.12) | data formatting | bytes 2097152 | tf_op jit(solution)/shard_map/reshape;squeeze | solution.py:532
  11.6 0.0 copy-done.12
  11.6 0.1 reduce_sum.9
  11.7 0.1 copy.22
  11.8 0.0 copy-done.7
  11.8 0.0 copy-done
  11.8 0.0 copy-done.1
  11.8 0.0 copy-done.2
  11.8 0.0 copy-start.3
  11.9 0.9 copy-done.3
  12.8 0.0 copy-start.4
  12.8 0.9 copy-done.4
  13.8 0.0 copy-start.5
  13.8 0.9 copy-done.5
  14.7 0.0 copy-start.6
  14.7 0.9 copy-done.6
  15.7 0.0 copy-start.8
  15.7 0.9 copy-done.8
  16.6 0.0 copy-start.9
  16.6 0.9 copy-done.9
  17.5 0.0 copy-start.10
  17.5 0.9 copy-done.10
  18.4 85.7 %join.1.joined = f32[4,64,256]{2,1,0:T(8,128)S(1)} custom-call(f32[4,256,256]{2,1,0:T(8,128)S(1)} %bitcast.9, f32[2,4,256,128]{3,2,1,0:T(8,128)S(1)} %bitcast.10, bf16[4,128,256]{2,1,0:T(8,128)(2,1)S(1)} %copy-done.3, bf16[4,128,256]{2,1,0:T(8,128)(2,1)S(1)} %copy-done.4, bf16[256,256]{1,0:T(8,128)(2,1)S(1)} %copy-done.7, bf16[256,256]{1,0:T(8,128)(2,1)S(1)} %copy-done.8, ...), custom_call_target="tpu_custom_call" | custom-call | tf_op jit(solution)/shard_map/join/pallas_call | solution.py:497
  104.1 0.1 copy_divide_fusion.taps
  104.2 0.0 all-to-all-done
  104.2 1.4 copy.31
  105.6 59.3 %deconvolve.1 = f32[4,64,256]{2,1,0:T(8,128)S(1)} custom-call(f32[4,3,9]{2,1,0:T(4,128)S(1)} %copy_divide_fusion.taps, f32[4,64,256]{2,1,0:T(8,128)S(1)} %join.1.joined, f32[4,4,64,256]{3,2,1,0:T(8,128)S(1)} %bitcast.11), custom_call_target="tpu_custom_call" | custom-call | tf_op jit(solution)/shard_map/deconvolve/pallas_call | solution.py:206
  164.9 0.7 copy.34
  165.6 0.7 copy.35
Async XLA Ops:
  3.5 5.0 %copy-start.11 = (f32[1,256,4,256]{3,2,1,0:T(4,128)S(1)}, f32[1,256,4,256]{3,2,1,0:T(4,128)}, u32[]{:S(2)}) copy-start(f32[1,256,4,256]{3,2,1,0:T(4,128)} %param.14) | copy-start | bytes 3145732
  3.5 100.6 %all-to-all-start = ((f32[1,4,256,256]{3,1,0,2:T(4,128)}), f32[1,4,256,256]{3,1,0,2:T(4,128)}, u32[]{:S(2)}, u32[]{:S(2)}) async-start(f32[1,4,256,256]{3,1,0,2:T(4,128)} %copy.24), calls=%async_computation | async-start | bytes 2097152 | tf_op jit(solution)/shard_map/all_to_all | solution.py:537
  8.5 3.1 %copy-start.12 = (f32[4,3,9]{2,0,1:T(4,128)S(1)}, f32[4,3,9]{2,0,1:T(4,128)}, u32[]{:S(2)}) copy-start(f32[4,3,9]{2,0,1:T(4,128)} %param.15) | copy-start | bytes 1300
  8.6 3.3 %copy-start.7 = (bf16[256,256]{1,0:T(8,128)(2,1)S(1)}, bf16[256,256]{1,0:T(8,128)(2,1)}, u32[]{:S(2)}) copy-start(bf16[256,256]{1,0:T(8,128)(2,1)} %constant.24.clone.dxh) | copy-start | bytes 393220
  9.9 1.9 %copy-start = (f32[1,4,256,256]{3,2,1,0:T(8,128)S(1)}, f32[1,4,256,256]{3,2,1,0:T(8,128)}, u32[]{:S(2)}) copy-start(f32[1,4,256,256]{3,2,1,0:T(8,128)} %param.13) | copy-start | bytes 3145732
  9.9 1.9 %copy-start.1 = (bf16[512,512]{1,0:T(8,128)(2,1)S(1)}, bf16[512,512]{1,0:T(8,128)(2,1)}, u32[]{:S(2)}) copy-start(bf16[512,512]{1,0:T(8,128)(2,1)} %constant.26.clone.mh) | copy-start | bytes 1572868
  9.9 1.9 %copy-start.2 = (bf16[512,512]{1,0:T(8,128)(2,1)S(1)}, bf16[512,512]{1,0:T(8,128)(2,1)}, u32[]{:S(2)}) copy-start(bf16[512,512]{1,0:T(8,128)(2,1)} %constant.27.clone.ml) | copy-start | bytes 1572868
  11.8 1.0 copy-start.3
  12.8 0.9 copy-start.4
  13.8 0.9 copy-start.5
  14.7 0.9 copy-start.6
  15.7 0.9 copy-start.8
  16.6 0.9 copy-start.9
  17.5 0.9 copy-start.10
where the time goes:
time: 167 us; the launch traced here: 166 us
  Pallas kernels  145 us (87%)
  local copies, waits for them, and re-layouts  15.4 us (9%)
  starting transfers between devices  5.01 us (3%)
    pallas_call x1, Pallas kernels, spectral_join(): pl.pallas_call(functools.partial(join_kernel, pencils), name='join', out_...  85.7 us
    pallas_call x1, Pallas kernels, richardson_lucy(): pl.pallas_call(functools.partial(rl_kernel, views, pencils), name='deconv...  59.3 us
    unnamed x30, local copies, waits for them, and re-layouts  12.2 us
    all_to_all x1, starting transfers between devices, body(): lax.all_to_all(recorded, 'view', split_axis=2, concat_axis=0, tiled=True)  5.01 us
  transfers between devices with their start and end apart: 1, of which 0 were waited for; matrix products, arithmetic and copies ran while one was open for 2% of the time, Pallas kernels for 52%

commit v1 on v0

v1 whole, which is shorter than its diff:
```python
import functools

import jax
import jax.numpy as jnp
import numpy as np
from jax import lax
from jax.experimental import pallas as pl
from jax.experimental.pallas import tpu as pltpu
from jax.sharding import PartitionSpec as P

ITERS = 2
MESH_ID = pl.DeviceIdType.MESH
F32 = jnp.float32
BF16 = jnp.bfloat16
SIDES = [(dv, dp) for dp in (-1, 1, 0) for dv in (0, -1, 1) if (dv, dp) != (0, 0)]
SLOT = {side: k for k, side in enumerate(SIDES)}


def halves(value):
    high = value.astype(BF16)
    return high, (value - high.astype(F32)).astype(BF16)


def dot(left, right):
    return jnp.dot(left, right, preferred_element_type=F32)


def two_terms(table):
    high = table.astype(jnp.bfloat16)
    low = (table - high.astype(np.float64)).astype(jnp.bfloat16)
    return [high, low]


def transform_tables(n, nx):
    at = np.arange(n)
    phase = 2.0 * np.pi * (at[:, None] * at[None, :] % n) / n
    cosine, sine = np.cos(phase), np.sin(phase)
    q = n // 4
    rows = np.concatenate([cosine.reshape(4, q, n), sine.reshape(4, q, n)], axis=1)

    x, c = np.arange(nx)[:, None], np.arange(nx // 2)[None, :]
    wave = 2.0 * np.pi * (x * c % nx) / nx
    sign = np.where(x % 2 == 0, 1.0, -1.0)
    columns = np.concatenate([np.cos(wave), np.where(c == 0, sign, -np.sin(wave))], axis=1)
    scale = 1.0 / (float(n) * n * nx)
    back_re = np.where(c == 0, 1.0, 2.0 * np.cos(wave)).T
    back_im = np.where(c == 0, sign, -2.0 * np.sin(wave)).T
    columns_back = np.concatenate([back_re, back_im], axis=0) * scale

    index = np.arange(2 * n)
    part, depth = index % 8 // 4, index // 8 * 4 + index % 4
    c_z, s_z = cosine[:, depth], sine[:, depth]
    depth_table = np.concatenate(
        [np.where(part == 0, c_z, s_z), np.where(part == 0, -s_z, c_z)], axis=0)

    m = np.arange(n // 2)
    back = []
    for core in range(2):
        ky = m // 2 * 4 + 2 * core + m % 2
        back.append(np.concatenate([cosine[:, ky], sine[:, ky]], axis=1))
    return [t for table in (rows, columns, depth_table, np.stack(back), columns_back)
            for t in two_terms(table)]


def right3(high, low, right):
    r_high, r_low = halves(right)
    return dot(high, r_high) + (dot(high, r_low) + dot(low, r_high))


def left3(left, high, low):
    l_high, l_low = halves(left)
    return dot(l_high, high) + (dot(l_high, low) + dot(l_low, high))


def reversal(n):
    total = lax.broadcasted_iota(jnp.int32, (n, n), 0) + lax.broadcasted_iota(jnp.int32, (n, n), 1)
    return jnp.where((total == 0) | (total == n), 1.0, 0.0).astype(BF16)


def moved_right(value, table):
    high, low = halves(value)
    return dot(high, table) + dot(low, table)


def moved_left(table, value):
    high, low = halves(value)
    return dot(table, high) + dot(table, low)


def dot3(left, right_high, right_low):
    high, low = halves(left)
    return dot(high, right_high) + (dot(high, right_low) + dot(low, right_high))


def kernel(views, pencils, taps, slab_ref, weight_ref, *refs):
    table_refs, refs = refs[:10], refs[10:]
    (out, out2, slab, weight, csh, csl, dxh, dxl, mh, ml, cyh, cyl, dih, dil,
     xh, xl, msg, got, wsend, wgot, we, wm, mth, mtl, g, gr, gm, fr, pj, r1, r2,
     stacked, est, zed, mid, spread, acc, rz, rs, th, tl, ah, al,
     ssem, rsem, lsem, load_sem, share_sem, send_sem, recv_sem) = refs
    n = 4 * pencils
    q = n // 4
    half = pencils // 2
    v, p = lax.axis_index("view"), lax.axis_index("pencil")
    core = lax.rem(v, 2)
    mate = v + 1 - 2 * core
    far = lax.rem(v + 2, 4)
    mirror = pencils - 1 - p
    mirror0 = lax.rem(pencils - p, pencils)
    own_mirror = (p == 0) | (p == half)

    tables = [csh, csl, dxh, dxl, mh, ml, cyh, cyl, dih, dil]
    loads = [pltpu.make_async_copy(src, dst, load_sem.at[k])
             for k, (src, dst) in enumerate(zip(table_refs, tables))]
    slab_load = pltpu.make_async_copy(slab_ref, slab, load_sem.at[10])
    weight_loads = [pltpu.make_async_copy(weight_ref.at[:, :, pl.ds(128 * h, 128)], weight.at[h], load_sem.at[11 + h])
                    for h in range(2)]
    slab_load.start()
    for load in loads[2:4] + weight_loads + loads[:2] + loads[4:]:
        load.start()
    flat = [weight.at[h].reshape(4 * n, 128) for h in range(2)]

    def weight_rows(h, j):
        return flat[h][pl.ds(j, n, stride=4), :]

    depth, rows, width = 4, q, slab.shape[-1]
    frame = rows + 16

    def exists(side):
        v1, p1 = v + side[0], p + side[1]
        return (v1 >= 0) & (v1 < views) & (p1 >= 0) & (p1 < pencils)

    def back(side):
        return (-side[0], -side[1])

    def each(sides, action):
        for side in sides:
            @pl.when(exists(side))
            def _(side=side):
                action(side)

    est[...] = jnp.zeros_like(est)
    rz[...] = jnp.zeros_like(rz)
    rs[...] = jnp.zeros_like(rs)

    barrier = pltpu.get_barrier_semaphore()

    def greet(i, carry):
        pl.semaphore_signal(barrier, inc=1, device_id=(v, lax.rem(p + i, pencils)), device_id_type=MESH_ID)
        return carry

    lax.fori_loop(1, pencils, greet, 0)
    for d in range(1, 4):
        pl.semaphore_signal(barrier, inc=1, device_id=(lax.rem(v + d, views), p), device_id_type=MESH_ID)
    corners = [side for side in SIDES if side[0] != 0 and side[1] != 0]

    def greet_corner(side):
        pl.semaphore_signal(barrier, inc=1, device_id=(v + side[0], p + side[1]), device_id_type=MESH_ID)

    each(corners, greet_corner)
    expected = pencils - 1 + 3 + sum(exists(side).astype(jnp.int32) for side in corners)

    slab_load.wait()
    loads[2].wait()
    loads[3].wait()
    for z in range(4):
        xh[z], xl[z] = halves(left3(slab[z], dxh[...], dxl[...]))
    mid[...] = jnp.zeros_like(mid)
    for load in weight_loads + loads[:2]:
        load.wait()

    def remote(src, dst, k, device):
        return pltpu.make_async_remote_copy(
            src_ref=src, dst_ref=dst, send_sem=ssem.at[k], recv_sem=rsem.at[k],
            device_id=device, device_id_type=MESH_ID)

    lane0 = lax.broadcasted_iota(jnp.int32, (n, 128), 1) == 0

    for j in range(4):
        receiver = mirror0 if j == 0 else mirror
        pick = lane0 & (receiver < half)
        wsend[j] = jnp.where(pick, weight_rows(0, j), weight_rows(1, j))

    pl.semaphore_wait(barrier, expected)
    w_rest = remote(wsend.at[pl.ds(1, 3)], wgot.at[pl.ds(1, 3)], 1, (v, mirror))
    w_first = remote(wsend.at[0], wgot.at[0], 2, (v, mirror0))
    w_local = pltpu.make_async_copy(wsend.at[0], wgot.at[0], lsem.at[0])
    w_rest.start()

    @pl.when(jnp.logical_not(own_mirror))
    def _():
        w_first.start()

    @pl.when(own_mirror)
    def _():
        w_local.start()

    lane_q = lax.broadcasted_iota(jnp.int32, (q, 128), 1) == 0
    row_q = lax.broadcasted_iota(jnp.int32, (q, 128), 0)

    group = pencils // 4
    for step in range(4):
        b = lax.rem(p // group + step, 4)
        first = b < 2
        for z in range(4):
            both = (dot(csh[b], xh[z]) + (dot(csh[b], xl[z]) + dot(csl[b], xh[z])))
            c_re, c_im = both[:q, :128], both[:q, 128:]
            s_re, s_im = both[q:, :128], both[q:, 128:]
            re, im = c_re + s_im, c_im - s_re
            re0 = jnp.where(first, c_re, c_im)
            im0 = jnp.where(first, -s_re, -s_im)
            im0 = jnp.where((row_q == 0) & (b == 0), c_im, im0)
            im0 = jnp.where((row_q == 0) & (b == 2), c_re, im0)
            at = pl.multiple_of(b * (q * 8), q * 8)
            msg[pl.ds(at + z, q, stride=8), :] = jnp.where(lane_q, re0, re)
            msg[pl.ds(at + 4 + z, q, stride=8), :] = jnp.where(lane_q, im0, im)

        def send_chunk(i, carry, b=b):
            peer = b * group + lax.rem(p + i, group)
            at = pl.multiple_of(peer * 32, 32)

            @pl.when(peer != p)
            def _():
                remote(msg.at[pl.ds(at, 32)], got.at[p], 0, (v, peer)).start()
            return carry

        lax.fori_loop(0, group, send_chunk, 0)

    own = pltpu.make_async_copy(msg.at[pl.ds(pl.multiple_of(p * 32, 32), 32)], got.at[p], lsem.at[1])
    own.start()

    def quarter_of(view):
        return slab.at[:, pl.ds(pl.multiple_of(view * q, q), q), :]

    shares = [pltpu.make_async_remote_copy(
        src_ref=quarter_of(lax.rem(v + d, views)), dst_ref=stacked.at[v],
        send_sem=share_sem.at[0, d - 1], recv_sem=share_sem.at[1, d - 1],
        device_id=(lax.rem(v + d, views), p), device_id_type=MESH_ID) for d in range(1, 4)]
    for share in shares:
        share.start()
    own_share = pltpu.make_async_copy(quarter_of(v), stacked.at[v], lsem.at[3])
    own_share.start()

    for load in loads[4:]:
        load.wait()
    mth[...] = mh[...].astype(F32).T.astype(BF16)
    mtl[...] = ml[...].astype(F32).T.astype(BF16)
    def band(v, carry):
        at = (lax.broadcasted_iota(jnp.int32, (width, width), 0)
              - lax.broadcasted_iota(jnp.int32, (width, width), 1))
        table, turned = jnp.zeros((width, width), F32), jnp.zeros((width, width), F32)
        for t in range(9):
            tap = taps[v, 2, t]
            table = jnp.where(at == t - 4, tap, table)
            turned = jnp.where(at == 4 - t, tap, turned)
        th[v], tl[v] = halves(table)
        ah[v], al[v] = halves(turned)
        return carry

    lax.fori_loop(0, views, band, 0)

    w_rest.wait_recv()

    @pl.when(jnp.logical_not(own_mirror))
    def _():
        w_first.wait_recv()

    @pl.when(own_mirror)
    def _():
        w_local.wait()

    turn_z, turn_x = reversal(n), reversal(128)
    for j in range(4):
        mine = jnp.where(lane0 & (p >= half), weight_rows(1, j), weight_rows(0, j))
        turned = moved_left(turn_z, moved_right(wgot[(4 - j) % 4], turn_x))
        we[j] = 0.5 * (mine + turned)

    @pl.when(own_mirror)
    def _():
        first = (lax.broadcasted_iota(jnp.int32, (n, 128), 0) * 0 + p) == 0
        other = jnp.where(first, weight_rows(1, 0), weight_rows(0, 0))
        other = 0.5 * (other + moved_left(turn_z, other))
        main = we[0]
        we[0] = jnp.where(lane0, 0.5 * (main + other), main)
        wm[...] = jnp.where(lane0, 0.5 * (main - other), 0.0)

    own.wait()
    remote(got.at[pl.ds(0, pencils - 1)], got.at[pl.ds(0, pencils - 1)], 0, (v, mirror)).wait_recv()

    def tile_rows(j):
        return got[:, 8 * j:8 * j + 8, :].reshape(2 * n, 128)

    for pair in range(2):
        f = right3(mh[...], ml[...], jnp.concatenate([tile_rows(2 * pair), tile_rows(2 * pair + 1)], axis=1))
        for k in range(2):
            j = 2 * pair + k
            for part in range(2):
                g[j, part * n:(part + 1) * n, :] = (
                    f[part * n:(part + 1) * n, 128 * k:128 * k + 128] * we[j])

    @pl.when(own_mirror)
    def _():
        imag = lax.rem(lax.broadcasted_iota(jnp.int32, (2 * n, 128), 0), 8) >= 4
        rows = tile_rows(0)
        f = right3(mh[...], ml[...], jnp.where(imag, -rows, rows))
        for part in range(2):
            g[0, part * n:(part + 1) * n, :] = (
                g[0, part * n:(part + 1) * n, :] + f[part * n:(part + 1) * n, :] * wm[...])

    pair_sum = remote(g.at[pl.ds(2 - 2 * core, 2)], gr, 3, (mate, p))
    pair_sum.start()
    pair_sum.wait_recv()
    f = right3(mth[...], mtl[...], jnp.concatenate(
        [g[2 * core] + gr[0], g[2 * core + 1] + gr[1]], axis=1))
    gm[:, 0:8, :] = f[:, :128].reshape(pencils, 8, 128)
    gm[:, 8:16, :] = f[:, 128:].reshape(pencils, 8, 128)

    def here(peer):
        return fr.at[pl.ds(pl.multiple_of(peer * 16, 16), 16)]

    def send_back(i, carry):
        peer = lax.rem(p + i, pencils)
        remote(gm.at[peer], here(p), 4, (v, peer)).start()
        return carry

    lax.fori_loop(1, pencils, send_back, 0)
    own_back = pltpu.make_async_copy(gm.at[p], here(p), lsem.at[2])
    own_back.start()
    own_back.wait()
    most = fr.at[pl.ds(0, 16 * (pencils - 1))]
    remote(most, most, 4, (v, mirror)).wait_recv()

    m = lax.broadcasted_iota(jnp.int32, (n // 2, 128), 0)
    ky = m // 2 * 4 + 2 * core + lax.rem(m, 2)
    lane_m = lax.broadcasted_iota(jnp.int32, (n // 2, 128), 1) == 0
    low, high = (ky > 0) & (ky < n // 2), ky > n // 2
    for z in range(4):
        re = fr[pl.ds(z, n // 2, stride=8), :]
        im = fr[pl.ds(4 + z, n // 2, stride=8), :]
        zero = jnp.zeros_like(re)
        v1 = jnp.where(low, 2.0 * re, jnp.where(ky == 0, re, jnp.where(ky == n // 2, im, zero)))
        v2 = jnp.where(high, 2.0 * re, jnp.where(ky == 0, im, jnp.where(ky == n // 2, re, zero)))
        b1 = jnp.where(low, -2.0 * im, zero)
        b2 = jnp.where(high, -2.0 * im, zero)
        top = jnp.concatenate([jnp.where(lane_m, v1, re), jnp.where(lane_m, v2, im)], axis=1)
        bottom = jnp.concatenate([jnp.where(lane_m, b1, -im), jnp.where(lane_m, b2, re)], axis=1)
        u = right3(cyh[core], cyl[core], jnp.concatenate([top, bottom], axis=0))
        field = left3(u, dih[...], dil[...])
        for quarter in range(4):
            pj[quarter // 2, quarter % 2, z] = field[quarter * q:(quarter + 1) * q]

    near = remote(pj.at[:, 1 - core], r1, 5, (mate, p))
    near.start()
    near.wait_recv()
    away = lax.rem(v // 2 + 1, 2)
    kept = v // 2
    r1[...] = r1[...] + pj[:, core]
    long = remote(r1.at[away], r2, 6, (far, p))
    long.start()
    long.wait_recv()
    out[...] = r1[kept] + r2[...]


    planes_of = {-1: pl.ds(0, depth), 0: pl.ds(depth, depth), 1: pl.ds(2 * depth, depth)}

    def est_copy(side):
        dv, dp = side
        src_rows = {0: pl.ds(8, rows), 1: pl.ds(rows, 8), -1: pl.ds(8, 8)}[dv]
        dst_rows = {0: pl.ds(8, rows), 1: pl.ds(0, 8), -1: pl.ds(rows + 8, 8)}[dv]
        return pltpu.make_async_remote_copy(
            src_ref=est.at[planes_of[0], :, src_rows, :],
            dst_ref=est.at[planes_of[-dp], :, dst_rows, :],
            send_sem=send_sem.at[0, SLOT[side]],
            recv_sem=recv_sem.at[0, SLOT[back(side)]],
            device_id=(v + dv, p + dp),
            device_id_type=MESH_ID,
        )

    def acc_copy(side):
        dv, dp = side
        src_rows = {0: pl.ds(8, rows), 1: pl.ds(rows + 8, 8), -1: pl.ds(0, 8)}[dv]
        slot = SLOT[back(side)]
        landing = rz.at[0 if dp == 1 else 1] if dv == 0 else rs.at[slot]
        return pltpu.make_async_remote_copy(
            src_ref=acc.at[planes_of[dp], :, src_rows, :],
            dst_ref=landing,
            send_sem=send_sem.at[1, SLOT[side]],
            recv_sem=recv_sem.at[1, slot],
            device_id=(v + dv, p + dp),
            device_id_type=MESH_ID,
        )

    def est_wait(side):
        dv, dp = side
        dst_rows = {0: pl.ds(8, rows), -1: pl.ds(0, 8), 1: pl.ds(rows + 8, 8)}[dv]
        landing = est.at[planes_of[dp], :, dst_rows, :]
        pltpu.make_async_remote_copy(
            src_ref=landing, dst_ref=landing, send_sem=send_sem.at[0, SLOT[side]],
            recv_sem=recv_sem.at[0, SLOT[side]], device_id=(v + dv, p + dp),
            device_id_type=MESH_ID).wait_recv()

    def acc_wait(side):
        dv, dp = side
        landing = rz.at[0 if dp == -1 else 1] if dv == 0 else rs.at[SLOT[side]]
        pltpu.make_async_remote_copy(
            src_ref=landing, dst_ref=landing, send_sem=send_sem.at[1, SLOT[side]],
            recv_sem=recv_sem.at[1, SLOT[side]], device_id=(v + dv, p + dp),
            device_id_type=MESH_ID).wait_recv()

    for h in range(2):
        s = out[:, :, h * 128:(h + 1) * 128]
        est[pl.ds(depth, depth), h, pl.ds(8, rows), :] = 0.1 + (
            jnp.maximum(s, 0.0) + jnp.log1p(jnp.exp(-jnp.abs(s))))

    each(SIDES, lambda side: est_copy(side).start())
    own_share.wait()
    for share in shares:
        share.wait_recv()

    def view_step(w, carry):
        for z in range(depth):
            total = taps[w, 0, 0] * est[z]
            for t in range(1, 9):
                total = total + taps[w, 0, t] * est[z + t]
            zed[z] = total
        sides = []
        for h in range(2):
            planes = []
            for z in range(depth):
                total = taps[w, 1, 0] * zed[z, h, pl.ds(4, rows), :]
                for t in range(1, 9):
                    total = total + taps[w, 1, t] * zed[z, h, pl.ds(4 + t, rows), :]
                planes.append(total)
            sides.append(jnp.concatenate(planes, axis=0))
        blurred = dot3(jnp.concatenate(sides, axis=1), th[w], tl[w])
        ratio = stacked[w].reshape(depth * rows, width) / blurred
        turned = dot3(ratio, ah[w], al[w])
        for z in range(depth):
            for h in range(2):
                mid[z, h, pl.ds(16, rows), :] = turned[z * rows:(z + 1) * rows, h * 128:(h + 1) * 128]
        for z in range(depth):
            for h in range(2):
                total = taps[w, 1, 8] * mid[z, h, pl.ds(4, frame), :]
                for t in range(1, 9):
                    total = total + taps[w, 1, 8 - t] * mid[z, h, pl.ds(4 + t, frame), :]
                spread[w, z, h] = total
        return carry

    def gather_planes(planes):
        for zo in planes:
            total = None
            for v in range(views):
                for zs in range(depth):
                    if 0 <= zo - zs <= 8:
                        term = taps[v, 0, zo - zs] * spread[v, zs]
                        total = term if total is None else total + term
            acc[zo] = total

    def iteration(step, carry):
        each(SIDES, est_wait)
        lax.fori_loop(0, views, view_step, 0)
        gather_planes(list(range(0, depth)) + list(range(2 * depth, 3 * depth)))
        each([s for s in SIDES if s[1] != 0], lambda side: acc_copy(side).start())
        gather_planes(range(depth, 2 * depth))
        each([s for s in SIDES if s[1] == 0], lambda side: acc_copy(side).start())
        each(SIDES, lambda side: est_copy(side).wait_send())
        each(SIDES, acc_wait)
        for z in range(depth):
            for h in range(2):
                total = acc[depth + z, h, pl.ds(8, rows), :] + (rz[0, z, h] + rz[1, z, h])
                low = rs[SLOT[(-1, 0)], z, h] + (rs[SLOT[(-1, -1)], z, h] + rs[SLOT[(-1, 1)], z, h])
                high = rs[SLOT[(1, 0)], z, h] + (rs[SLOT[(1, -1)], z, h] + rs[SLOT[(1, 1)], z, h])
                total = jnp.concatenate(
                    [total[:8] + low, total[8:rows - 8], total[rows - 8:] + high], axis=0)
                fresh = est[depth + z, h, pl.ds(8, rows), :] * (total * (1.0 / views))
                est[depth + z, h, pl.ds(8, rows), :] = fresh
        each(SIDES, lambda side: acc_copy(side).wait_send())

        @pl.when(step < ITERS - 1)
        def _():
            each(SIDES, lambda side: est_copy(side).start())
        return carry

    lax.fori_loop(0, ITERS, iteration, 0)
    for h in range(2):
        out2[:, :, h * 128:(h + 1) * 128] = est[pl.ds(depth, depth), h, pl.ds(8, rows), :]

    w_rest.wait_send()
    sent = msg.at[pl.ds(0, 32 * (pencils - 1))]
    remote(sent, sent, 0, (v, mirror)).wait_send()
    pair_sum.wait_send()
    sent_back = gm.at[pl.ds(0, pencils - 1)]
    remote(sent_back, sent_back, 4, (v, mirror)).wait_send()
    near.wait_send()
    long.wait_send()

    @pl.when(jnp.logical_not(own_mirror))
    def _():
        w_first.wait_send()
    for share in shares:
        share.wait_send()


def whole(recorded, weight, taps):
    views, pencils = lax.axis_size("view"), lax.axis_size("pencil")
    n, nx = 4 * pencils, recorded.shape[-1]
    q, depth = n // 4, 4
    frame = q + 16
    vmem, left = pl.BlockSpec(memory_space=pltpu.VMEM), pl.BlockSpec(memory_space=pl.ANY)
    tables = [jnp.asarray(t) for t in transform_tables(n, nx)]
    block = jax.ShapeDtypeStruct((depth, q, nx), F32)
    return pl.pallas_call(
        functools.partial(kernel, views, pencils),
        name="join_and_deconvolve",
        out_shape=(block, block),
        in_specs=[pl.BlockSpec(memory_space=pltpu.SMEM)] + [left] * (2 + len(tables)),
        out_specs=(vmem, vmem),
        scratch_shapes=[
            pltpu.VMEM((4, n, nx), F32),
            pltpu.VMEM((2, n, 4, 128), F32),
            *[pltpu.VMEM(t.shape, t.dtype) for t in tables],
            pltpu.VMEM((4, n, nx), BF16),
            pltpu.VMEM((4, n, nx), BF16),
            pltpu.VMEM((8 * n, 128), F32),
            pltpu.VMEM((pencils, 32, 128), F32),
            pltpu.VMEM((4, n, 128), F32),
            pltpu.VMEM((4, n, 128), F32),
            pltpu.VMEM((4, n, 128), F32),
            pltpu.VMEM((n, 128), F32),
            pltpu.VMEM((2 * n, 2 * n), BF16),
            pltpu.VMEM((2 * n, 2 * n), BF16),
            pltpu.VMEM((4, 2 * n, 128), F32),
            pltpu.VMEM((2, 2 * n, 128), F32),
            pltpu.VMEM((pencils, 16, 128), F32),
            pltpu.VMEM((pencils * 16, 128), F32),
            pltpu.VMEM((2, 2, 4, q, nx), F32),
            pltpu.VMEM((2, 4, q, nx), F32),
            pltpu.VMEM((4, q, nx), F32),
            pltpu.VMEM((views, depth, q, nx), F32),
            pltpu.VMEM((3 * depth, 2, frame, 128), F32),
            pltpu.VMEM((depth, 2, frame, 128), F32),
            pltpu.VMEM((depth, 2, frame + 16, 128), F32),
            pltpu.VMEM((views, depth, 2, frame, 128), F32),
            pltpu.VMEM((3 * depth, 2, frame, 128), F32),
            pltpu.VMEM((2, depth, 2, q, 128), F32),
            pltpu.VMEM((8, depth, 2, 8, 128), F32),
            *[pltpu.VMEM((views, nx, nx), BF16)] * 4,
            pltpu.SemaphoreType.DMA((7,)),
            pltpu.SemaphoreType.DMA((7,)),
            pltpu.SemaphoreType.DMA((4,)),
            pltpu.SemaphoreType.DMA((13,)),
            pltpu.SemaphoreType.DMA((2, 3)),
            pltpu.SemaphoreType.DMA((2, 8)),
            pltpu.SemaphoreType.DMA((2, 8)),
        ],
        compiler_params=pltpu.CompilerParams(collective_id=1, has_side_effects=True,
                                             vmem_limit_bytes=48 * 1024 * 1024),
    )(taps, recorded, weight, *tables)


def body(recorded, spectral_weight, psf_taps):
    kernels = psf_taps / jnp.sum(psf_taps, axis=-1, keepdims=True)
    return whole(recorded[0], spectral_weight[0], kernels)


def solution(mesh):
    return jax.shard_map(
        body,
        mesh=mesh,
        in_specs=(P("view", "pencil", None, None), P("view", None, "pencil", None), P()),
        out_specs=(P("pencil", "view", None), P("pencil", "view", None)),
        check_vma=False,
    )
```

time: 167 us -> 160 us (0.958)
  starting transfers between devices: 5.01 us -> 0 us
  local copies, waits for them, and re-layouts: 15.4 us -> 13.5 us
    all_to_all x1 -> x0, starting transfers between devices: 5.01 us -> none  [body(): lax.all_to_all(recorded, 'view', split_axis=2, concat_axis=0, tiled=True)]
    another operation x1 -> x0, local copies, waits for them, and re-layouts: 1.7 us -> none  [weight_halves(): return jnp.transpose(block.reshape(n, chunk, 2, nx // 2), (2, 1, 0, 3))]
    unnamed x30 -> x28, local copies, waits for them, and re-layouts: 12.2 us -> 13.4 us
    pallas_call x2 -> x1, Pallas kernels: 145 us -> 144 us  [whole(): pl.pallas_call(functools.partial(kernel, views, pencils), name='join_and_...]
  transfers between devices with their start and end apart: 1 -> 0, of which waited for: 0 -> 0; matrix products, arithmetic and copies ran while one was open for 2% -> 0% of each run, Pallas kernels for 52% -> 0%
where the time goes in v1:
time: 160 us; the launch traced here: 159 us
  Pallas kernels  144 us (90%)
  local copies, waits for them, and re-layouts  13.5 us (8%)
    pallas_call x1, Pallas kernels, whole(): pl.pallas_call(functools.partial(kernel, views, pencils), name='join_and_...  144 us
    unnamed x28, local copies, waits for them, and re-layouts  13.4 us

profile of v1, /device:TPU:3, one launch (start us, length us, event | category | flops | bytes accessed | tf_op | source)
XLA Modules:
  0.0 159.3 jit_solution(12023719939350336541)
XLA Ops:
  0.6 0.0 copy-start.12
  0.6 0.8 reduce_sum.9
  1.5 0.1 copy.16
  1.6 0.0 copy-done.12
  1.6 0.1 copy_divide_fusion.taps
  1.7 0.0 copy-start
  1.7 1.2 copy-done
  2.9 0.0 copy-start.1
  2.9 1.2 copy-done.1
  4.1 0.0 copy-start.2
  4.1 1.0 copy-done.2
  5.2 0.0 copy-start.3
  5.2 1.0 copy-done.3
  6.2 0.0 copy-start.4
  6.2 0.9 copy-done.4
  7.1 0.0 copy-start.5
  7.1 0.9 copy-done.5
  8.1 0.0 copy-start.6
  8.1 0.9 copy-done.6
  9.0 0.0 copy-start.7
  9.1 0.9 copy-done.7
  10.0 0.0 copy-start.8
  10.0 0.9 copy-done.8
  10.9 0.0 copy-start.9
  10.9 0.9 copy-done.9
  11.8 0.0 copy-start.10
  11.8 0.9 copy-done.10
  12.7 0.0 copy-start.11
  12.7 0.9 copy-done.11
  13.6 144.3 %join_and_deconvolve.1 = (f32[4,64,256]{2,1,0:T(8,128)S(1)}, f32[4,64,256]{2,1,0:T(8,128)S(1)}) custom-call(f32[4,3,9]{2,1,0:T(4,128)S(1)} %copy_divide_fusion.taps, f32[4,256,256]{2,1,0:T(8,128)S(1)} %bitcast.2, f32[256,4,256]{2,1,0:T(4,128)S(1)} %bitcast.3, bf16[4,128,256]{2,1,0:T(8,128)(2,1)S(1)} %copy-done.7, bf16[4,128,256]{2,1,0:T(8,128)(2,1)S(1)} %copy-done.6, ...), custom_call_target="tpu_custom_call" | custom-call | tf_op jit(solution)/shard_map/join_and_deconvolve/pallas_call | solution.py:512
  157.9 0.7 copy.21
  158.6 0.7 copy.22
Async XLA Ops:
  0.6 1.0 copy-start.12
  1.7 1.2 copy-start
  2.9 1.2 copy-start.1
  4.1 1.0 copy-start.2
  5.2 1.0 copy-start.3
  6.2 0.9 copy-start.4
  7.1 0.9 copy-start.5
  8.1 0.9 copy-start.6
  9.0 0.9 copy-start.7
  10.0 0.9 copy-start.8
  10.9 0.9 copy-start.9
  11.8 0.9 copy-start.10
  12.7 0.9 copy-start.11

commit v2 on v1

--- a/solution.py
+++ b/solution.py
@@ -9,6 +9,7 @@
 from jax.sharding import PartitionSpec as P
 
 ITERS = 2
+UNROLL = 4
 MESH_ID = pl.DeviceIdType.MESH
 F32 = jnp.float32
 BF16 = jnp.bfloat16
@@ -95,7 +96,7 @@
 def kernel(views, pencils, taps, slab_ref, weight_ref, *refs):
     table_refs, refs = refs[:10], refs[10:]
     (out, out2, slab, weight, csh, csl, dxh, dxl, mh, ml, cyh, cyl, dih, dil,
-     xh, xl, msg, got, wsend, wgot, we, wm, mth, mtl, g, gr, gm, fr, pj, r1, r2,
+     xh, xl, msg, got, wsend, wgot, we, wm, mth, mtl, g, gr, fs, gm, fr, pj, r1, r2,
      stacked, est, zed, mid, spread, acc, rz, rs, th, tl, ah, al,
      ssem, rsem, lsem, load_sem, share_sem, send_sem, recv_sem) = refs
     n = 4 * pencils
@@ -150,15 +151,21 @@
         return carry
 
     lax.fori_loop(1, pencils, greet, 0)
-    for d in range(1, 4):
-        pl.semaphore_signal(barrier, inc=1, device_id=(lax.rem(v + d, views), p), device_id_type=MESH_ID)
+
+    def greet_far(i, carry):
+        pl.semaphore_signal(barrier, inc=1, device_id=(far, lax.rem(p + i, pencils)), device_id_type=MESH_ID)
+        return carry
+
+    lax.fori_loop(0, pencils, greet_far, 0)
+    for other in (mate, lax.rem(mate + 2, 4)):
+        pl.semaphore_signal(barrier, inc=1, device_id=(other, p), device_id_type=MESH_ID)
     corners = [side for side in SIDES if side[0] != 0 and side[1] != 0]
 
     def greet_corner(side):
         pl.semaphore_signal(barrier, inc=1, device_id=(v + side[0], p + side[1]), device_id_type=MESH_ID)
 
     each(corners, greet_corner)
-    expected = pencils - 1 + 3 + sum(exists(side).astype(jnp.int32) for side in corners)
+    expected = 2 * pencils + 1 + sum(exists(side).astype(jnp.int32) for side in corners)
 
     slab_load.wait()
     loads[2].wait()
@@ -312,31 +319,45 @@
     pair_sum.wait_recv()
     f = right3(mth[...], mtl[...], jnp.concatenate(
         [g[2 * core] + gr[0], g[2 * core + 1] + gr[1]], axis=1))
-    gm[:, 0:8, :] = f[:, :128].reshape(pencils, 8, 128)
-    gm[:, 8:16, :] = f[:, 128:].reshape(pencils, 8, 128)
-
-    def here(peer):
-        return fr.at[pl.ds(pl.multiple_of(peer * 16, 16), 16)]
+    kept = v // 2
+    away = 1 - kept
+    for k in range(2):
+        fs[k] = f[:, 128 * k:128 * k + 128]
+    for x in range(2):
+        for k in range(2):
+            for part in range(2):
+                for zz in range(2):
+                    gm[x, pl.ds(4 * k + 2 * part + zz, pencils, stride=8), :] = (
+                        fs[k, pl.ds(4 * part + 2 * x + zz, pencils, stride=8), :])
+
+    def rows_of(peer):
+        return pl.ds(pl.multiple_of(peer * 8, 8), 8)
 
     def send_back(i, carry):
         peer = lax.rem(p + i, pencils)
-        remote(gm.at[peer], here(p), 4, (v, peer)).start()
+
+        @pl.when(i > 0)
+        def _():
+            remote(gm.at[kept, rows_of(peer)], fr.at[kept, rows_of(p)], 4, (v, peer)).start()
+
+        remote(gm.at[away, rows_of(peer)], fr.at[kept, rows_of(p)], 7, (far, peer)).start()
         return carry
 
-    lax.fori_loop(1, pencils, send_back, 0)
-    own_back = pltpu.make_async_copy(gm.at[p], here(p), lsem.at[2])
+    lax.fori_loop(0, pencils, send_back, 0)
+    own_back = pltpu.make_async_copy(gm.at[kept, rows_of(p)], fr.at[kept, rows_of(p)], lsem.at[2])
     own_back.start()
     own_back.wait()
-    most = fr.at[pl.ds(0, 16 * (pencils - 1))]
+    most = fr.at[kept, pl.ds(0, 8 * (pencils - 1))]
     remote(most, most, 4, (v, mirror)).wait_recv()
+    remote(fr.at[away], fr.at[away], 7, (far, p)).wait_recv()
 
     m = lax.broadcasted_iota(jnp.int32, (n // 2, 128), 0)
     ky = m // 2 * 4 + 2 * core + lax.rem(m, 2)
     lane_m = lax.broadcasted_iota(jnp.int32, (n // 2, 128), 1) == 0
     low, high = (ky > 0) & (ky < n // 2), ky > n // 2
-    for z in range(4):
-        re = fr[pl.ds(z, n // 2, stride=8), :]
-        im = fr[pl.ds(4 + z, n // 2, stride=8), :]
+    for zz in range(2):
+        re = fr[0, pl.ds(zz, n // 2, stride=4), :] + fr[1, pl.ds(zz, n // 2, stride=4), :]
+        im = fr[0, pl.ds(2 + zz, n // 2, stride=4), :] + fr[1, pl.ds(2 + zz, n // 2, stride=4), :]
         zero = jnp.zeros_like(re)
         v1 = jnp.where(low, 2.0 * re, jnp.where(ky == 0, re, jnp.where(ky == n // 2, im, zero)))
         v2 = jnp.where(high, 2.0 * re, jnp.where(ky == 0, im, jnp.where(ky == n // 2, re, zero)))
@@ -347,18 +368,17 @@
         u = right3(cyh[core], cyl[core], jnp.concatenate([top, bottom], axis=0))
         field = left3(u, dih[...], dil[...])
         for quarter in range(4):
-            pj[quarter // 2, quarter % 2, z] = field[quarter * q:(quarter + 1) * q]
+            pj[quarter // 2, quarter % 2, zz] = field[quarter * q:(quarter + 1) * q]
 
     near = remote(pj.at[:, 1 - core], r1, 5, (mate, p))
     near.start()
     near.wait_recv()
-    away = lax.rem(v // 2 + 1, 2)
-    kept = v // 2
     r1[...] = r1[...] + pj[:, core]
     long = remote(r1.at[away], r2, 6, (far, p))
     long.start()
     long.wait_recv()
-    out[...] = r1[kept] + r2[...]
+    out[pl.ds(2 * kept, 2)] = r1[kept]
+    out[pl.ds(2 * away, 2)] = r2[...]
 
 
     planes_of = {-1: pl.ds(0, depth), 0: pl.ds(depth, depth), 1: pl.ds(2 * depth, depth)}
@@ -422,14 +442,14 @@
             total = taps[w, 0, 0] * est[z]
             for t in range(1, 9):
                 total = total + taps[w, 0, t] * est[z + t]
-            zed[z] = total
+            zed[w, z] = total
         sides = []
         for h in range(2):
             planes = []
             for z in range(depth):
-                total = taps[w, 1, 0] * zed[z, h, pl.ds(4, rows), :]
+                total = taps[w, 1, 0] * zed[w, z, h, pl.ds(4, rows), :]
                 for t in range(1, 9):
-                    total = total + taps[w, 1, t] * zed[z, h, pl.ds(4 + t, rows), :]
+                    total = total + taps[w, 1, t] * zed[w, z, h, pl.ds(4 + t, rows), :]
                 planes.append(total)
             sides.append(jnp.concatenate(planes, axis=0))
         blurred = dot3(jnp.concatenate(sides, axis=1), th[w], tl[w])
@@ -437,12 +457,12 @@
         turned = dot3(ratio, ah[w], al[w])
         for z in range(depth):
             for h in range(2):
-                mid[z, h, pl.ds(16, rows), :] = turned[z * rows:(z + 1) * rows, h * 128:(h + 1) * 128]
+                mid[w, z, h, pl.ds(16, rows), :] = turned[z * rows:(z + 1) * rows, h * 128:(h + 1) * 128]
         for z in range(depth):
             for h in range(2):
-                total = taps[w, 1, 8] * mid[z, h, pl.ds(4, frame), :]
+                total = taps[w, 1, 8] * mid[w, z, h, pl.ds(4, frame), :]
                 for t in range(1, 9):
-                    total = total + taps[w, 1, 8 - t] * mid[z, h, pl.ds(4 + t, frame), :]
+                    total = total + taps[w, 1, 8 - t] * mid[w, z, h, pl.ds(4 + t, frame), :]
                 spread[w, z, h] = total
         return carry
 
@@ -458,7 +478,7 @@
 
     def iteration(step, carry):
         each(SIDES, est_wait)
-        lax.fori_loop(0, views, view_step, 0)
+        lax.fori_loop(0, views, view_step, 0, unroll=UNROLL)
         gather_planes(list(range(0, depth)) + list(range(2 * depth, 3 * depth)))
         each([s for s in SIDES if s[1] != 0], lambda side: acc_copy(side).start())
         gather_planes(range(depth, 2 * depth))
@@ -489,8 +509,9 @@
     sent = msg.at[pl.ds(0, 32 * (pencils - 1))]
     remote(sent, sent, 0, (v, mirror)).wait_send()
     pair_sum.wait_send()
-    sent_back = gm.at[pl.ds(0, pencils - 1)]
+    sent_back = gm.at[kept, pl.ds(0, 8 * (pencils - 1))]
     remote(sent_back, sent_back, 4, (v, mirror)).wait_send()
+    remote(gm.at[away], gm.at[away], 7, (far, p)).wait_send()
     near.wait_send()
     long.wait_send()
 
@@ -506,7 +527,7 @@
     n, nx = 4 * pencils, recorded.shape[-1]
     q, depth = n // 4, 4
     frame = q + 16
-    vmem, left = pl.BlockSpec(memory_space=pltpu.VMEM), pl.BlockSpec(memory_space=pl.ANY)
+    vmem, left = pl.BlockSpec(memory_space=pltpu.VMEM), pl.BlockSpec(memory_space=pltpu.HBM)
     tables = [jnp.asarray(t) for t in transform_tables(n, nx)]
     block = jax.ShapeDtypeStruct((depth, q, nx), F32)
     return pl.pallas_call(
@@ -531,22 +552,23 @@
             pltpu.VMEM((2 * n, 2 * n), BF16),
             pltpu.VMEM((4, 2 * n, 128), F32),
             pltpu.VMEM((2, 2 * n, 128), F32),
-            pltpu.VMEM((pencils, 16, 128), F32),
-            pltpu.VMEM((pencils * 16, 128), F32),
-            pltpu.VMEM((2, 2, 4, q, nx), F32),
-            pltpu.VMEM((2, 4, q, nx), F32),
-            pltpu.VMEM((4, q, nx), F32),
+            pltpu.VMEM((2, 2 * n, 128), F32),
+            pltpu.VMEM((2, 8 * pencils, 128), F32),
+            pltpu.VMEM((2, 8 * pencils, 128), F32),
+            pltpu.VMEM((2, 2, 2, q, nx), F32),
+            pltpu.VMEM((2, 2, q, nx), F32),
+            pltpu.VMEM((2, q, nx), F32),
             pltpu.VMEM((views, depth, q, nx), F32),
             pltpu.VMEM((3 * depth, 2, frame, 128), F32),
-            pltpu.VMEM((depth, 2, frame, 128), F32),
-            pltpu.VMEM((depth, 2, frame + 16, 128), F32),
+            pltpu.VMEM((views, depth, 2, frame, 128), F32),
+            pltpu.VMEM((views, depth, 2, frame + 16, 128), F32),
             pltpu.VMEM((views, depth, 2, frame, 128), F32),
             pltpu.VMEM((3 * depth, 2, frame, 128), F32),
             pltpu.VMEM((2, depth, 2, q, 128), F32),
             pltpu.VMEM((8, depth, 2, 8, 128), F32),
             *[pltpu.VMEM((views, nx, nx), BF16)] * 4,
-            pltpu.SemaphoreType.DMA((7,)),
-            pltpu.SemaphoreType.DMA((7,)),
+            pltpu.SemaphoreType.DMA((8,)),
+            pltpu.SemaphoreType.DMA((8,)),
             pltpu.SemaphoreType.DMA((4,)),
             pltpu.SemaphoreType.DMA((13,)),
             pltpu.SemaphoreType.DMA((2, 3)),
@@ -554,7 +576,7 @@
             pltpu.SemaphoreType.DMA((2, 8)),
         ],
         compiler_params=pltpu.CompilerParams(collective_id=1, has_side_effects=True,
-                                             vmem_limit_bytes=48 * 1024 * 1024),
+                                             vmem_limit_bytes=60 * 1024 * 1024),
     )(taps, recorded, weight, *tables)
 
 

time: 160 us -> 145 us (0.906)
  the two profiles are of different devices: /device:TPU:3 before, /device:TPU:2 now
where the time goes in v2:
time: 145 us
  Pallas kernels  140 us (97%)
  local copies, waits for them, and re-layouts  2.52 us (2%)
  other arithmetic  1.52 us (1%)
    pallas_call x1, Pallas kernels, whole(): pl.pallas_call(functools.partial(kernel, views, pencils), name='join_and_...  140 us

profile of v2, /device:TPU:2, one launch (start us, length us, event | category | flops | bytes accessed | tf_op | source)
XLA Modules:
  0.0 144.7 jit_solution(664534256444420710)
XLA Ops:
  0.6 0.0 copy-start.1
  0.6 0.8 reduce_sum.9
  1.5 0.1 copy.16
  1.6 0.0 copy-done.1
  1.6 0.7 copy_divide_fusion.taps
  2.3 140.0 %join_and_deconvolve.1 = (f32[4,64,256]{2,1,0:T(8,128)}, f32[4,64,256]{2,1,0:T(8,128)}) custom-call(f32[4,3,9]{2,1,0:T(4,128)} %copy_divide_fusion.taps, f32[4,256,256]{2,1,0:T(8,128)} %bitcast.2, f32[256,4,256]{2,1,0:T(4,128)} %bitcast.3, bf16[4,128,256]{2,1,0:T(8,128)(2,1)} %constant.22.clone.refs_0_, bf16[4,128,256]{2,1,0:T(8,128)(2,1)} %constant.23.clone.refs_1_, ...), custom_call_target="tpu_custom_call" | custom-call | tf_op jit(solution)/shard_map/join_and_deconvolve/pallas_call | solution.py:533
  142.3 0.0 copy-start
  142.3 1.7 %copy.21 = f32[4,64,256]{2,1,0:T(8,128)} copy(f32[4,64,256]{2,1,0:T(8,128)} %get-tuple-element.4) | data formatting | bytes 524288
  144.0 0.0 copy-done
  144.0 0.7 copy.22
Async XLA Ops:
  0.6 1.0 copy-start.1
  142.3 1.7 %copy-start = (f32[4,64,256]{2,1,0:T(8,128)S(1)}, f32[4,64,256]{2,1,0:T(8,128)}, u32[]{:S(2)}) copy-start(f32[4,64,256]{2,1,0:T(8,128)} %get-tuple-element.5) | copy-start | bytes 786436

commit v3 on v2

--- a/solution.py
+++ b/solution.py
@@ -96,7 +96,7 @@
 def kernel(views, pencils, taps, slab_ref, weight_ref, *refs):
     table_refs, refs = refs[:10], refs[10:]
     (out, out2, slab, weight, csh, csl, dxh, dxl, mh, ml, cyh, cyl, dih, dil,
-     xh, xl, msg, got, wsend, wgot, we, wm, mth, mtl, g, gr, fs, gm, fr, pj, r1, r2,
+     xh, xl, msg, got, wsend, wgot, we, wm, mth, mtl, g, gr, gsh, gsl, fs, gm, fr, pj, r1, r2,
      stacked, est, zed, mid, spread, acc, rz, rs, th, tl, ah, al,
      ssem, rsem, lsem, load_sem, share_sem, send_sem, recv_sem) = refs
     n = 4 * pencils
@@ -260,8 +260,14 @@
             tap = taps[v, 2, t]
             table = jnp.where(at == t - 4, tap, table)
             turned = jnp.where(at == 4 - t, tap, turned)
-        th[v], tl[v] = halves(table)
-        ah[v], al[v] = halves(turned)
+        whole_sum = 1.0
+        for axis in range(3):
+            axis_sum = taps[v, axis, 0]
+            for t in range(1, 9):
+                axis_sum = axis_sum + taps[v, axis, t]
+            whole_sum = whole_sum * axis_sum
+        th[v], tl[v] = halves(table / whole_sum)
+        ah[v], al[v] = halves(turned / whole_sum)
         return carry
 
     lax.fori_loop(0, views, band, 0)
@@ -294,56 +300,68 @@
     own.wait()
     remote(got.at[pl.ds(0, pencils - 1)], got.at[pl.ds(0, pencils - 1)], 0, (v, mirror)).wait_recv()
 
-    def tile_rows(j):
-        return got[:, 8 * j:8 * j + 8, :].reshape(2 * n, 128)
-
-    for pair in range(2):
-        f = right3(mh[...], ml[...], jnp.concatenate([tile_rows(2 * pair), tile_rows(2 * pair + 1)], axis=1))
+    def pair_spectra(pair):
+        block = got[:, pl.ds(pl.multiple_of(16 * pair, 16), 16), :]
+        return [block[:, 8 * k:8 * k + 8, :].reshape(2 * n, 128) for k in range(2)]
+
+    def weigh(pair):
+        f = right3(mh[...], ml[...], jnp.concatenate(pair_spectra(pair), axis=1))
         for k in range(2):
             j = 2 * pair + k
             for part in range(2):
                 g[j, part * n:(part + 1) * n, :] = (
                     f[part * n:(part + 1) * n, 128 * k:128 * k + 128] * we[j])
 
-    @pl.when(own_mirror)
-    def _():
-        imag = lax.rem(lax.broadcasted_iota(jnp.int32, (2 * n, 128), 0), 8) >= 4
-        rows = tile_rows(0)
-        f = right3(mh[...], ml[...], jnp.where(imag, -rows, rows))
-        for part in range(2):
-            g[0, part * n:(part + 1) * n, :] = (
-                g[0, part * n:(part + 1) * n, :] + f[part * n:(part + 1) * n, :] * wm[...])
-
+        @pl.when(own_mirror & (pair == 0))
+        def _():
+            imag = lax.rem(lax.broadcasted_iota(jnp.int32, (2 * n, 128), 0), 8) >= 4
+            lines = got[:, 0:8, :].reshape(2 * n, 128)
+            f = right3(mh[...], ml[...], jnp.where(imag, -lines, lines))
+            for part in range(2):
+                g[0, part * n:(part + 1) * n, :] = (
+                    g[0, part * n:(part + 1) * n, :] + f[part * n:(part + 1) * n, :] * wm[...])
+
+    weigh(1 - core)
     pair_sum = remote(g.at[pl.ds(2 - 2 * core, 2)], gr, 3, (mate, p))
     pair_sum.start()
+    weigh(core)
     pair_sum.wait_recv()
-    f = right3(mth[...], mtl[...], jnp.concatenate(
+    gsh[...], gsl[...] = halves(jnp.concatenate(
         [g[2 * core] + gr[0], g[2 * core + 1] + gr[1]], axis=1))
+
     kept = v // 2
     away = 1 - kept
-    for k in range(2):
-        fs[k] = f[:, 128 * k:128 * k + 128]
-    for x in range(2):
-        for k in range(2):
-            for part in range(2):
-                for zz in range(2):
-                    gm[x, pl.ds(4 * k + 2 * part + zz, pencils, stride=8), :] = (
-                        fs[k, pl.ds(4 * part + 2 * x + zz, pencils, stride=8), :])
 
     def rows_of(peer):
         return pl.ds(pl.multiple_of(peer * 8, 8), 8)
 
-    def send_back(i, carry):
-        peer = lax.rem(p + i, pencils)
-
-        @pl.when(i > 0)
-        def _():
-            remote(gm.at[kept, rows_of(peer)], fr.at[kept, rows_of(p)], 4, (v, peer)).start()
-
-        remote(gm.at[away, rows_of(peer)], fr.at[kept, rows_of(p)], 7, (far, peer)).start()
-        return carry
-
-    lax.fori_loop(0, pencils, send_back, 0)
+    for step in range(2):
+        b = lax.rem(p // half + step, 2)
+        at = pl.multiple_of(b * n, n)
+        block = pl.ds(at, n)
+        f = (dot(mth[block, :], gsh[...])
+             + (dot(mth[block, :], gsl[...]) + dot(mtl[block, :], gsh[...])))
+        for k in range(2):
+            fs[k, block, :] = f[:, 128 * k:128 * k + 128]
+        for x in range(2):
+            for k in range(2):
+                for part in range(2):
+                    for zz in range(2):
+                        gm[x, pl.ds(at + (4 * k + 2 * part + zz), half, stride=8), :] = (
+                            fs[k, pl.ds(at + (4 * part + 2 * x + zz), half, stride=8), :])
+
+        def send_back(i, carry, b=b):
+            peer = b * half + lax.rem(p + i, half)
+
+            @pl.when(peer != p)
+            def _():
+                remote(gm.at[kept, rows_of(peer)], fr.at[kept, rows_of(p)], 4, (v, peer)).start()
+
+            remote(gm.at[away, rows_of(peer)], fr.at[kept, rows_of(p)], 7, (far, peer)).start()
+            return carry
+
+        lax.fori_loop(0, half, send_back, 0)
+
     own_back = pltpu.make_async_copy(gm.at[kept, rows_of(p)], fr.at[kept, rows_of(p)], lsem.at[2])
     own_back.start()
     own_back.wait()
@@ -376,63 +394,70 @@
     r1[...] = r1[...] + pj[:, core]
     long = remote(r1.at[away], r2, 6, (far, p))
     long.start()
-    long.wait_recv()
-    out[pl.ds(2 * kept, 2)] = r1[kept]
-    out[pl.ds(2 * away, 2)] = r2[...]
-
-
-    planes_of = {-1: pl.ds(0, depth), 0: pl.ds(depth, depth), 1: pl.ds(2 * depth, depth)}
-
-    def est_copy(side):
+
+    def est_copy(side, z):
         dv, dp = side
         src_rows = {0: pl.ds(8, rows), 1: pl.ds(rows, 8), -1: pl.ds(8, 8)}[dv]
         dst_rows = {0: pl.ds(8, rows), 1: pl.ds(0, 8), -1: pl.ds(rows + 8, 8)}[dv]
         return pltpu.make_async_remote_copy(
-            src_ref=est.at[planes_of[0], :, src_rows, :],
-            dst_ref=est.at[planes_of[-dp], :, dst_rows, :],
-            send_sem=send_sem.at[0, SLOT[side]],
-            recv_sem=recv_sem.at[0, SLOT[back(side)]],
+            src_ref=est.at[depth + z, :, src_rows, :],
+            dst_ref=est.at[depth * (1 - dp) + z, :, dst_rows, :],
+            send_sem=send_sem.at[0, SLOT[side], z],
+            recv_sem=recv_sem.at[0, SLOT[back(side)], z],
             device_id=(v + dv, p + dp),
             device_id_type=MESH_ID,
         )
 
-    def acc_copy(side):
+    def acc_copy(side, z):
         dv, dp = side
         src_rows = {0: pl.ds(8, rows), 1: pl.ds(rows + 8, 8), -1: pl.ds(0, 8)}[dv]
         slot = SLOT[back(side)]
-        landing = rz.at[0 if dp == 1 else 1] if dv == 0 else rs.at[slot]
+        landing = rz.at[0 if dp == 1 else 1, z] if dv == 0 else rs.at[slot, z]
         return pltpu.make_async_remote_copy(
-            src_ref=acc.at[planes_of[dp], :, src_rows, :],
+            src_ref=acc.at[depth * (1 + dp) + z, :, src_rows, :],
             dst_ref=landing,
-            send_sem=send_sem.at[1, SLOT[side]],
-            recv_sem=recv_sem.at[1, slot],
+            send_sem=send_sem.at[1, SLOT[side], z],
+            recv_sem=recv_sem.at[1, slot, z],
             device_id=(v + dv, p + dp),
             device_id_type=MESH_ID,
         )
 
-    def est_wait(side):
+    def est_wait(side, z):
         dv, dp = side
         dst_rows = {0: pl.ds(8, rows), -1: pl.ds(0, 8), 1: pl.ds(rows + 8, 8)}[dv]
-        landing = est.at[planes_of[dp], :, dst_rows, :]
+        landing = est.at[depth * (1 + dp) + z, :, dst_rows, :]
         pltpu.make_async_remote_copy(
-            src_ref=landing, dst_ref=landing, send_sem=send_sem.at[0, SLOT[side]],
-            recv_sem=recv_sem.at[0, SLOT[side]], device_id=(v + dv, p + dp),
+            src_ref=landing, dst_ref=landing, send_sem=send_sem.at[0, SLOT[side], z],
+            recv_sem=recv_sem.at[0, SLOT[side], z], device_id=(v + dv, p + dp),
             device_id_type=MESH_ID).wait_recv()
 
-    def acc_wait(side):
+    def acc_wait(side, z):
         dv, dp = side
-        landing = rz.at[0 if dp == -1 else 1] if dv == 0 else rs.at[SLOT[side]]
+        landing = rz.at[0 if dp == -1 else 1, z] if dv == 0 else rs.at[SLOT[side], z]
         pltpu.make_async_remote_copy(
-            src_ref=landing, dst_ref=landing, send_sem=send_sem.at[1, SLOT[side]],
-            recv_sem=recv_sem.at[1, SLOT[side]], device_id=(v + dv, p + dp),
+            src_ref=landing, dst_ref=landing, send_sem=send_sem.at[1, SLOT[side], z],
+            recv_sem=recv_sem.at[1, SLOT[side], z], device_id=(v + dv, p + dp),
             device_id_type=MESH_ID).wait_recv()
 
-    for h in range(2):
-        s = out[:, :, h * 128:(h + 1) * 128]
-        est[pl.ds(depth, depth), h, pl.ds(8, rows), :] = 0.1 + (
-            jnp.maximum(s, 0.0) + jnp.log1p(jnp.exp(-jnp.abs(s))))
-
-    each(SIDES, lambda side: est_copy(side).start())
+    def every_plane(action):
+        def at_plane(z, carry):
+            each(SIDES, lambda side: action(side, z))
+            return carry
+
+        lax.fori_loop(0, depth, at_plane, 0)
+
+    def start_estimate(first, planes):
+        out[pl.ds(first, 2)] = planes
+        for h in range(2):
+            s = planes[:, :, h * 128:(h + 1) * 128]
+            est[pl.ds(depth + first, 2), h, pl.ds(8, rows), :] = 0.1 + (
+                jnp.maximum(s, 0.0) + jnp.log1p(jnp.exp(-jnp.abs(s))))
+        for zz in range(2):
+            each(SIDES, lambda side: est_copy(side, first + zz).start())
+
+    start_estimate(2 * kept, r1[kept])
+    long.wait_recv()
+    start_estimate(2 * away, r2[...])
     own_share.wait()
     for share in shares:
         share.wait_recv()
@@ -477,28 +502,31 @@
             acc[zo] = total
 
     def iteration(step, carry):
-        each(SIDES, est_wait)
+        every_plane(est_wait)
         lax.fori_loop(0, views, view_step, 0, unroll=UNROLL)
-        gather_planes(list(range(0, depth)) + list(range(2 * depth, 3 * depth)))
-        each([s for s in SIDES if s[1] != 0], lambda side: acc_copy(side).start())
-        gather_planes(range(depth, 2 * depth))
-        each([s for s in SIDES if s[1] == 0], lambda side: acc_copy(side).start())
-        each(SIDES, lambda side: est_copy(side).wait_send())
-        each(SIDES, acc_wait)
         for z in range(depth):
+            gather_planes([z, 2 * depth + z, depth + z])
+            each(SIDES, lambda side: acc_copy(side, z).start())
+
+        def finish_plane(z, carry):
+            each(SIDES, lambda side: acc_wait(side, z))
+            each(SIDES, lambda side: est_copy(side, z).wait_send())
             for h in range(2):
                 total = acc[depth + z, h, pl.ds(8, rows), :] + (rz[0, z, h] + rz[1, z, h])
                 low = rs[SLOT[(-1, 0)], z, h] + (rs[SLOT[(-1, -1)], z, h] + rs[SLOT[(-1, 1)], z, h])
                 high = rs[SLOT[(1, 0)], z, h] + (rs[SLOT[(1, -1)], z, h] + rs[SLOT[(1, 1)], z, h])
                 total = jnp.concatenate(
                     [total[:8] + low, total[8:rows - 8], total[rows - 8:] + high], axis=0)
-                fresh = est[depth + z, h, pl.ds(8, rows), :] * (total * (1.0 / views))
-                est[depth + z, h, pl.ds(8, rows), :] = fresh
-        each(SIDES, lambda side: acc_copy(side).wait_send())
-
-        @pl.when(step < ITERS - 1)
-        def _():
-            each(SIDES, lambda side: est_copy(side).start())
+                est[depth + z, h, pl.ds(8, rows), :] = (
+                    est[depth + z, h, pl.ds(8, rows), :] * (total * (1.0 / views)))
+
+            @pl.when(step < ITERS - 1)
+            def _():
+                each(SIDES, lambda side: est_copy(side, z).start())
+            return carry
+
+        lax.fori_loop(0, depth, finish_plane, 0)
+        every_plane(lambda side, z: acc_copy(side, z).wait_send())
         return carry
 
     lax.fori_loop(0, ITERS, iteration, 0)
@@ -552,6 +580,8 @@
             pltpu.VMEM((2 * n, 2 * n), BF16),
             pltpu.VMEM((4, 2 * n, 128), F32),
             pltpu.VMEM((2, 2 * n, 128), F32),
+            pltpu.VMEM((2 * n, 256), BF16),
+            pltpu.VMEM((2 * n, 256), BF16),
             pltpu.VMEM((2, 2 * n, 128), F32),
             pltpu.VMEM((2, 8 * pencils, 128), F32),
             pltpu.VMEM((2, 8 * pencils, 128), F32),
@@ -572,8 +602,8 @@
             pltpu.SemaphoreType.DMA((4,)),
             pltpu.SemaphoreType.DMA((13,)),
             pltpu.SemaphoreType.DMA((2, 3)),
-            pltpu.SemaphoreType.DMA((2, 8)),
-            pltpu.SemaphoreType.DMA((2, 8)),
+            pltpu.SemaphoreType.DMA((2, 8, 4)),
+            pltpu.SemaphoreType.DMA((2, 8, 4)),
         ],
         compiler_params=pltpu.CompilerParams(collective_id=1, has_side_effects=True,
                                              vmem_limit_bytes=60 * 1024 * 1024),
@@ -581,8 +611,7 @@
 
 
 def body(recorded, spectral_weight, psf_taps):
-    kernels = psf_taps / jnp.sum(psf_taps, axis=-1, keepdims=True)
-    return whole(recorded[0], spectral_weight[0], kernels)
+    return whole(recorded[0], spectral_weight[0], psf_taps)
 
 
 def solution(mesh):

time: 145 us -> 141 us (0.972)
  the two profiles are of different devices: /device:TPU:2 before, /device:TPU:25 now
where the time goes in v3:
time: 141 us
  Pallas kernels  136 us (96%)
  local copies, waits for them, and re-layouts  3.72 us (3%)
    pallas_call x1, Pallas kernels, whole(): pl.pallas_call(functools.partial(kernel, views, pencils), name='join_and_...  136 us
    unnamed x5, local copies, waits for them, and re-layouts  3.72 us

profile of v3, /device:TPU:25, one launch (start us, length us, event | category | flops | bytes accessed | tf_op | source)
XLA Modules:
  0.0 140.8 jit_solution(17313903955755415672)
XLA Ops:
  0.6 1.3 copy.15.taps
  1.9 136.4 %join_and_deconvolve.1 = (f32[4,64,256]{2,1,0:T(8,128)}, f32[4,64,256]{2,1,0:T(8,128)}) custom-call(f32[4,3,9]{2,1,0:T(4,128)} %copy.15.taps, f32[4,256,256]{2,1,0:T(8,128)} %bitcast.2, f32[256,4,256]{2,1,0:T(4,128)} %bitcast.3, bf16[4,128,256]{2,1,0:T(8,128)(2,1)} %constant.20.clone.refs_0_, bf16[4,128,256]{2,1,0:T(8,128)(2,1)} %constant.21.clone.refs_1_, ...), custom_call_target="tpu_custom_call" | custom-call | tf_op jit(solution)/shard_map/join_and_deconvolve/pallas_call | solution.py:561
  138.3 0.0 copy-start
  138.4 1.7 %copy.18 = f32[4,64,256]{2,1,0:T(8,128)} copy(f32[4,64,256]{2,1,0:T(8,128)} %get-tuple-element.4) | data formatting | bytes 524288
  140.1 0.0 copy-done
  140.1 0.7 copy.19
Async XLA Ops:
  138.3 1.7 %copy-start = (f32[4,64,256]{2,1,0:T(8,128)S(1)}, f32[4,64,256]{2,1,0:T(8,128)}, u32[]{:S(2)}) copy-start(f32[4,64,256]{2,1,0:T(8,128)} %get-tuple-element.5) | copy-start | bytes 786436

commit v4 on v3

--- a/solution.py
+++ b/solution.py
@@ -150,13 +150,13 @@
         pl.semaphore_signal(barrier, inc=1, device_id=(v, lax.rem(p + i, pencils)), device_id_type=MESH_ID)
         return carry
 
-    lax.fori_loop(1, pencils, greet, 0)
+    lax.fori_loop(1, pencils, greet, 0, unroll=7)
 
     def greet_far(i, carry):
         pl.semaphore_signal(barrier, inc=1, device_id=(far, lax.rem(p + i, pencils)), device_id_type=MESH_ID)
         return carry
 
-    lax.fori_loop(0, pencils, greet_far, 0)
+    lax.fori_loop(0, pencils, greet_far, 0, unroll=8)
     for other in (mate, lax.rem(mate + 2, 4)):
         pl.semaphore_signal(barrier, inc=1, device_id=(other, p), device_id_type=MESH_ID)
     corners = [side for side in SIDES if side[0] != 0 and side[1] != 0]
@@ -231,7 +231,7 @@
                 remote(msg.at[pl.ds(at, 32)], got.at[p], 0, (v, peer)).start()
             return carry
 
-        lax.fori_loop(0, group, send_chunk, 0)
+        lax.fori_loop(0, group, send_chunk, 0, unroll=2)
 
     own = pltpu.make_async_copy(msg.at[pl.ds(pl.multiple_of(p * 32, 32), 32)], got.at[p], lsem.at[1])
     own.start()
@@ -257,14 +257,14 @@
               - lax.broadcasted_iota(jnp.int32, (width, width), 1))
         table, turned = jnp.zeros((width, width), F32), jnp.zeros((width, width), F32)
         for t in range(9):
-            tap = taps[v, 2, t]
+            tap = taps[2, v, t]
             table = jnp.where(at == t - 4, tap, table)
             turned = jnp.where(at == 4 - t, tap, turned)
         whole_sum = 1.0
         for axis in range(3):
-            axis_sum = taps[v, axis, 0]
+            axis_sum = taps[axis, v, 0]
             for t in range(1, 9):
-                axis_sum = axis_sum + taps[v, axis, t]
+                axis_sum = axis_sum + taps[axis, v, t]
             whole_sum = whole_sum * axis_sum
         th[v], tl[v] = halves(table / whole_sum)
         ah[v], al[v] = halves(turned / whole_sum)
@@ -360,7 +360,7 @@
             remote(gm.at[away, rows_of(peer)], fr.at[kept, rows_of(p)], 7, (far, peer)).start()
             return carry
 
-        lax.fori_loop(0, half, send_back, 0)
+        lax.fori_loop(0, half, send_back, 0, unroll=2)
 
     own_back = pltpu.make_async_copy(gm.at[kept, rows_of(p)], fr.at[kept, rows_of(p)], lsem.at[2])
     own_back.start()
@@ -387,13 +387,18 @@
         field = left3(u, dih[...], dil[...])
         for quarter in range(4):
             pj[quarter // 2, quarter % 2, zz] = field[quarter * q:(quarter + 1) * q]
-
-    near = remote(pj.at[:, 1 - core], r1, 5, (mate, p))
-    near.start()
-    near.wait_recv()
-    r1[...] = r1[...] + pj[:, core]
-    long = remote(r1.at[away], r2, 6, (far, p))
-    long.start()
+        remote(pj.at[:, 1 - core, zz], r1.at[:, zz], 5 + 3 * zz, (mate, p)).start()
+
+    def near(zz):
+        return remote(pj.at[:, 1 - core, zz], r1.at[:, zz], 5 + 3 * zz, (mate, p))
+
+    def long(zz):
+        return remote(r1.at[away, zz], r2.at[zz], 6 + 3 * zz, (far, p))
+
+    for zz in range(2):
+        near(zz).wait_recv()
+        r1[:, zz] = r1[:, zz] + pj[:, core, zz]
+        long(zz).start()
 
     def est_copy(side, z):
         dv, dp = side
@@ -446,35 +451,36 @@
 
         lax.fori_loop(0, depth, at_plane, 0)
 
-    def start_estimate(first, planes):
-        out[pl.ds(first, 2)] = planes
+    def start_estimate(z, plane):
+        out[z] = plane
         for h in range(2):
-            s = planes[:, :, h * 128:(h + 1) * 128]
-            est[pl.ds(depth + first, 2), h, pl.ds(8, rows), :] = 0.1 + (
-                jnp.maximum(s, 0.0) + jnp.log1p(jnp.exp(-jnp.abs(s))))
-        for zz in range(2):
-            each(SIDES, lambda side: est_copy(side, first + zz).start())
-
-    start_estimate(2 * kept, r1[kept])
-    long.wait_recv()
-    start_estimate(2 * away, r2[...])
+            half_plane = plane[:, h * 128:(h + 1) * 128]
+            est[depth + z, h, pl.ds(8, rows), :] = 0.1 + (
+                jnp.maximum(half_plane, 0.0) + jnp.log1p(jnp.exp(-jnp.abs(half_plane))))
+        each(SIDES, lambda side: est_copy(side, z).start())
+
+    for zz in range(2):
+        start_estimate(2 * kept + zz, r1[kept, zz])
+    for zz in range(2):
+        long(zz).wait_recv()
+        start_estimate(2 * away + zz, r2[zz])
     own_share.wait()
     for share in shares:
         share.wait_recv()
 
     def view_step(w, carry):
         for z in range(depth):
-            total = taps[w, 0, 0] * est[z]
+            total = taps[0, w, 0] * est[z]
             for t in range(1, 9):
-                total = total + taps[w, 0, t] * est[z + t]
+                total = total + taps[0, w, t] * est[z + t]
             zed[w, z] = total
         sides = []
         for h in range(2):
             planes = []
             for z in range(depth):
-                total = taps[w, 1, 0] * zed[w, z, h, pl.ds(4, rows), :]
+                total = taps[1, w, 0] * zed[w, z, h, pl.ds(4, rows), :]
                 for t in range(1, 9):
-                    total = total + taps[w, 1, t] * zed[w, z, h, pl.ds(4 + t, rows), :]
+                    total = total + taps[1, w, t] * zed[w, z, h, pl.ds(4 + t, rows), :]
                 planes.append(total)
             sides.append(jnp.concatenate(planes, axis=0))
         blurred = dot3(jnp.concatenate(sides, axis=1), th[w], tl[w])
@@ -485,9 +491,9 @@
                 mid[w, z, h, pl.ds(16, rows), :] = turned[z * rows:(z + 1) * rows, h * 128:(h + 1) * 128]
         for z in range(depth):
             for h in range(2):
-                total = taps[w, 1, 8] * mid[w, z, h, pl.ds(4, frame), :]
+                total = taps[1, w, 8] * mid[w, z, h, pl.ds(4, frame), :]
                 for t in range(1, 9):
-                    total = total + taps[w, 1, 8 - t] * mid[w, z, h, pl.ds(4 + t, frame), :]
+                    total = total + taps[1, w, 8 - t] * mid[w, z, h, pl.ds(4 + t, frame), :]
                 spread[w, z, h] = total
         return carry
 
@@ -497,7 +503,7 @@
             for v in range(views):
                 for zs in range(depth):
                     if 0 <= zo - zs <= 8:
-                        term = taps[v, 0, zo - zs] * spread[v, zs]
+                        term = taps[0, v, zo - zs] * spread[v, zs]
                         total = term if total is None else total + term
             acc[zo] = total
 
@@ -540,8 +546,9 @@
     sent_back = gm.at[kept, pl.ds(0, 8 * (pencils - 1))]
     remote(sent_back, sent_back, 4, (v, mirror)).wait_send()
     remote(gm.at[away], gm.at[away], 7, (far, p)).wait_send()
-    near.wait_send()
-    long.wait_send()
+    for zz in range(2):
+        near(zz).wait_send()
+        long(zz).wait_send()
 
     @pl.when(jnp.logical_not(own_mirror))
     def _():
@@ -557,7 +564,7 @@
     frame = q + 16
     vmem, left = pl.BlockSpec(memory_space=pltpu.VMEM), pl.BlockSpec(memory_space=pltpu.HBM)
     tables = [jnp.asarray(t) for t in transform_tables(n, nx)]
-    block = jax.ShapeDtypeStruct((depth, q, nx), F32)
+    block = pltpu.VMEM((depth, q, nx), F32)
     return pl.pallas_call(
         functools.partial(kernel, views, pencils),
         name="join_and_deconvolve",
@@ -597,8 +604,8 @@
             pltpu.VMEM((2, depth, 2, q, 128), F32),
             pltpu.VMEM((8, depth, 2, 8, 128), F32),
             *[pltpu.VMEM((views, nx, nx), BF16)] * 4,
-            pltpu.SemaphoreType.DMA((8,)),
-            pltpu.SemaphoreType.DMA((8,)),
+            pltpu.SemaphoreType.DMA((10,)),
+            pltpu.SemaphoreType.DMA((10,)),
             pltpu.SemaphoreType.DMA((4,)),
             pltpu.SemaphoreType.DMA((13,)),
             pltpu.SemaphoreType.DMA((2, 3)),
@@ -606,12 +613,35 @@
             pltpu.SemaphoreType.DMA((2, 8, 4)),
         ],
         compiler_params=pltpu.CompilerParams(collective_id=1, has_side_effects=True,
-                                             vmem_limit_bytes=60 * 1024 * 1024),
+                                             vmem_limit_bytes=62 * 1024 * 1024),
     )(taps, recorded, weight, *tables)
 
 
+def store(first, second, first_out, second_out, sem):
+    copies = [pltpu.make_async_copy(src, dst, sem.at[k])
+              for k, (src, dst) in enumerate(((first, first_out), (second, second_out)))]
+    for copy in copies:
+        copy.start()
+    for copy in copies:
+        copy.wait()
+
+
+def stored(first, second):
+    shape = jax.ShapeDtypeStruct(first.shape, F32)
+    return pl.pallas_call(
+        store,
+        name="store",
+        out_shape=(shape, shape),
+        in_specs=[pl.BlockSpec(memory_space=pl.ANY)] * 2,
+        out_specs=(pl.BlockSpec(memory_space=pltpu.HBM),) * 2,
+        scratch_shapes=[pltpu.SemaphoreType.DMA((2,))],
+        compiler_params=pltpu.CompilerParams(vmem_limit_bytes=2 * 1024 * 1024),
+    )(first, second)
+
+
 def body(recorded, spectral_weight, psf_taps):
-    return whole(recorded[0], spectral_weight[0], psf_taps)
+    taps = jnp.transpose(psf_taps, (1, 0, 2))
+    return stored(*whole(recorded[0], spectral_weight[0], taps))
 
 
 def solution(mesh):

time: 141 us -> 136 us (0.965)
  local copies, waits for them, and re-layouts: 3.72 us -> 0 us
    unnamed x5 -> x0, local copies, waits for them, and re-layouts: 3.72 us -> none
    pallas_call x1, Pallas kernels: 136 us -> 134 us  [whole(): pl.pallas_call(functools.partial(kernel, views, pencils), name='join_and_...]
where the time goes in v4:
time: 136 us; the launch traced here: 135 us
  Pallas kernels  135 us (99%)
    pallas_call x1, Pallas kernels, whole(): pl.pallas_call(functools.partial(kernel, views, pencils), name='join_and_...  134 us

profile of v4, /device:TPU:25, one launch (start us, length us, event | category | flops | bytes accessed | tf_op | source)
XLA Modules:
  0.0 135.5 jit_solution(1983537808477008784)
XLA Ops:
  0.6 134.0 %join_and_deconvolve.1 = (f32[4,64,256]{2,1,0:T(8,128)S(1)}, f32[4,64,256]{2,1,0:T(8,128)S(1)}) custom-call(f32[3,4,9]{2,1,0:T(4,128)} %bitcast.5, f32[4,256,256]{2,1,0:T(8,128)} %bitcast.3, f32[256,4,256]{2,1,0:T(4,128)} %bitcast.4, bf16[4,128,256]{2,1,0:T(8,128)(2,1)} %constant.20.clone.refs_0_, bf16[4,128,256]{2,1,0:T(8,128)(2,1)} %constant.21.clone.refs_1_, ...), custom_call_target="tpu_custom_call" | custom-call | tf_op jit(solution)/shard_map/join_and_deconvolve/pallas_call | solution.py:568
  134.7 0.8 store.1

commit v5 on v4

--- a/solution.py
+++ b/solution.py
@@ -10,6 +10,7 @@
 
 ITERS = 2
 UNROLL = 4
+LATE = (3, 7, 11)
 MESH_ID = pl.DeviceIdType.MESH
 F32 = jnp.float32
 BF16 = jnp.bfloat16
@@ -444,12 +445,12 @@
             recv_sem=recv_sem.at[1, SLOT[side], z], device_id=(v + dv, p + dp),
             device_id_type=MESH_ID).wait_recv()
 
-    def every_plane(action):
+    def every_plane(action, planes):
         def at_plane(z, carry):
             each(SIDES, lambda side: action(side, z))
             return carry
 
-        lax.fori_loop(0, depth, at_plane, 0)
+        lax.fori_loop(0, planes, at_plane, 0)
 
     def start_estimate(z, plane):
         out[z] = plane
@@ -468,11 +469,22 @@
     for share in shares:
         share.wait_recv()
 
+    def early_step(w, carry):
+        for z in range(depth):
+            total = None
+            for t in range(9):
+                if z + t not in LATE:
+                    term = taps[0, w, t] * est[z + t]
+                    total = term if total is None else total + term
+            zed[w, z] = total
+        return carry
+
     def view_step(w, carry):
         for z in range(depth):
-            total = taps[0, w, 0] * est[z]
-            for t in range(1, 9):
-                total = total + taps[0, w, t] * est[z + t]
+            total = zed[w, z]
+            for plane in LATE:
+                if 0 <= plane - z <= 8:
+                    total = total + taps[0, w, plane - z] * est[plane]
             zed[w, z] = total
         sides = []
         for h in range(2):
@@ -508,7 +520,9 @@
             acc[zo] = total
 
     def iteration(step, carry):
-        every_plane(est_wait)
+        every_plane(est_wait, depth - 1)
+        lax.fori_loop(0, views, early_step, 0)
+        each(SIDES, lambda side: est_wait(side, depth - 1))
         lax.fori_loop(0, views, view_step, 0, unroll=UNROLL)
         for z in range(depth):
             gather_planes([z, 2 * depth + z, depth + z])
@@ -532,7 +546,7 @@
             return carry
 
         lax.fori_loop(0, depth, finish_plane, 0)
-        every_plane(lambda side, z: acc_copy(side, z).wait_send())
+        every_plane(lambda side, z: acc_copy(side, z).wait_send(), depth)
         return carry
 
     lax.fori_loop(0, ITERS, iteration, 0)

time: 136 us -> 135 us (level)
  no operation moved by 1% of the time
where the time goes in v5:
time: 135 us
  Pallas kernels  134 us (99%)
    pallas_call x1, Pallas kernels, whole(): pl.pallas_call(functools.partial(kernel, views, pencils), name='join_and_...  133 us

profile of v5, /device:TPU:25, one launch (start us, length us, event | category | flops | bytes accessed | tf_op | source)
XLA Modules:
  0.0 134.6 jit_solution(17295645200682966544)
XLA Ops:
  0.6 133.1 %join_and_deconvolve.1 = (f32[4,64,256]{2,1,0:T(8,128)S(1)}, f32[4,64,256]{2,1,0:T(8,128)S(1)}) custom-call(f32[3,4,9]{2,1,0:T(4,128)} %bitcast.5, f32[4,256,256]{2,1,0:T(8,128)} %bitcast.3, f32[256,4,256]{2,1,0:T(4,128)} %bitcast.4, bf16[4,128,256]{2,1,0:T(8,128)(2,1)} %constant.20.clone.refs_0_, bf16[4,128,256]{2,1,0:T(8,128)(2,1)} %constant.21.clone.refs_1_, ...), custom_call_target="tpu_custom_call" | custom-call | tf_op jit(solution)/shard_map/join_and_deconvolve/pallas_call | solution.py:582
  133.8 0.8 store.1

commit v6 on v5

--- a/solution.py
+++ b/solution.py
@@ -98,7 +98,7 @@
     table_refs, refs = refs[:10], refs[10:]
     (out, out2, slab, weight, csh, csl, dxh, dxl, mh, ml, cyh, cyl, dih, dil,
      xh, xl, msg, got, wsend, wgot, we, wm, mth, mtl, g, gr, gsh, gsl, fs, gm, fr, pj, r1, r2,
-     stacked, est, zed, mid, spread, acc, rz, rs, th, tl, ah, al,
+     stacked, est, zed, mid, spread, acc, rz, rs, es, er, cs, strip, th, tl, ah, al,
      ssem, rsem, lsem, load_sem, share_sem, send_sem, recv_sem) = refs
     n = 4 * pencils
     q = n // 4
@@ -315,12 +315,9 @@
 
         @pl.when(own_mirror & (pair == 0))
         def _():
-            imag = lax.rem(lax.broadcasted_iota(jnp.int32, (2 * n, 128), 0), 8) >= 4
-            lines = got[:, 0:8, :].reshape(2 * n, 128)
-            f = right3(mh[...], ml[...], jnp.where(imag, -lines, lines))
-            for part in range(2):
-                g[0, part * n:(part + 1) * n, :] = (
-                    g[0, part * n:(part + 1) * n, :] + f[part * n:(part + 1) * n, :] * wm[...])
+            turned = moved_left(turn_z, jnp.concatenate([f[:n, :128], f[n:, :128]], axis=1))
+            g[0, :n, :] = g[0, :n, :] + turned[:, :128] * wm[...]
+            g[0, n:, :] = g[0, n:, :] - turned[:, 128:] * wm[...]
 
     weigh(1 - core)
     pair_sum = remote(g.at[pl.ds(2 - 2 * core, 2)], gr, 3, (mate, p))
@@ -403,11 +400,10 @@
 
     def est_copy(side, z):
         dv, dp = side
-        src_rows = {0: pl.ds(8, rows), 1: pl.ds(rows, 8), -1: pl.ds(8, 8)}[dv]
-        dst_rows = {0: pl.ds(8, rows), 1: pl.ds(0, 8), -1: pl.ds(rows + 8, 8)}[dv]
+        own_rows = pl.ds(8, rows)
         return pltpu.make_async_remote_copy(
-            src_ref=est.at[depth + z, :, src_rows, :],
-            dst_ref=est.at[depth * (1 - dp) + z, :, dst_rows, :],
+            src_ref=es.at[(dv + 1) // 2, z] if dv else est.at[depth + z, :, own_rows, :],
+            dst_ref=er.at[SLOT[back(side)], z] if dv else est.at[depth * (1 - dp) + z, :, own_rows, :],
             send_sem=send_sem.at[0, SLOT[side], z],
             recv_sem=recv_sem.at[0, SLOT[back(side)], z],
             device_id=(v + dv, p + dp),
@@ -416,11 +412,10 @@
 
     def acc_copy(side, z):
         dv, dp = side
-        src_rows = {0: pl.ds(8, rows), 1: pl.ds(rows + 8, 8), -1: pl.ds(0, 8)}[dv]
         slot = SLOT[back(side)]
         landing = rz.at[0 if dp == 1 else 1, z] if dv == 0 else rs.at[slot, z]
         return pltpu.make_async_remote_copy(
-            src_ref=acc.at[depth * (1 + dp) + z, :, src_rows, :],
+            src_ref=cs.at[(dv + 1) // 2, dp + 1, z] if dv else acc.at[depth * (1 + dp) + z, :, pl.ds(8, rows), :],
             dst_ref=landing,
             send_sem=send_sem.at[1, SLOT[side], z],
             recv_sem=recv_sem.at[1, slot, z],
@@ -430,12 +425,15 @@
 
     def est_wait(side, z):
         dv, dp = side
-        dst_rows = {0: pl.ds(8, rows), -1: pl.ds(0, 8), 1: pl.ds(rows + 8, 8)}[dv]
-        landing = est.at[depth * (1 + dp) + z, :, dst_rows, :]
+        plane = depth * (1 + dp) + z
+        landing = er.at[SLOT[side], z] if dv else est.at[plane, :, pl.ds(8, rows), :]
         pltpu.make_async_remote_copy(
             src_ref=landing, dst_ref=landing, send_sem=send_sem.at[0, SLOT[side], z],
             recv_sem=recv_sem.at[0, SLOT[side], z], device_id=(v + dv, p + dp),
             device_id_type=MESH_ID).wait_recv()
+        if dv:
+            for h in range(2):
+                est[plane, h, pl.ds(4 if dv < 0 else rows + 8, 4), :] = er[SLOT[side], z, pl.ds(4 * h, 4), :]
 
     def acc_wait(side, z):
         dv, dp = side
@@ -445,6 +443,20 @@
             recv_sem=recv_sem.at[1, SLOT[side], z], device_id=(v + dv, p + dp),
             device_id_type=MESH_ID).wait_recv()
 
+    def send_estimate(z):
+        for h in range(2):
+            es[0, z, pl.ds(4 * h, 4), :] = est[depth + z, h, pl.ds(8, 4), :]
+            es[1, z, pl.ds(4 * h, 4), :] = est[depth + z, h, pl.ds(rows + 4, 4), :]
+        each(SIDES, lambda side: est_copy(side, z).start())
+
+    def send_correction(z):
+        for dp in (-1, 0, 1):
+            for h in range(2):
+                plane = depth * (1 + dp) + z
+                cs[0, dp + 1, z, pl.ds(4 * h, 4), :] = acc[plane, h, pl.ds(4, 4), :]
+                cs[1, dp + 1, z, pl.ds(4 * h, 4), :] = acc[plane, h, pl.ds(rows + 8, 4), :]
+        each(SIDES, lambda side: acc_copy(side, z).start())
+
     def every_plane(action, planes):
         def at_plane(z, carry):
             each(SIDES, lambda side: action(side, z))
@@ -458,7 +470,7 @@
             half_plane = plane[:, h * 128:(h + 1) * 128]
             est[depth + z, h, pl.ds(8, rows), :] = 0.1 + (
                 jnp.maximum(half_plane, 0.0) + jnp.log1p(jnp.exp(-jnp.abs(half_plane))))
-        each(SIDES, lambda side: est_copy(side, z).start())
+        send_estimate(z)
 
     for zz in range(2):
         start_estimate(2 * kept + zz, r1[kept, zz])
@@ -526,23 +538,24 @@
         lax.fori_loop(0, views, view_step, 0, unroll=UNROLL)
         for z in range(depth):
             gather_planes([z, 2 * depth + z, depth + z])
-            each(SIDES, lambda side: acc_copy(side, z).start())
+            send_correction(z)
 
         def finish_plane(z, carry):
             each(SIDES, lambda side: acc_wait(side, z))
             each(SIDES, lambda side: est_copy(side, z).wait_send())
+            for end in (-1, 1):
+                strip[...] = rs[SLOT[(end, 0)], z] + (rs[SLOT[(end, -1)], z] + rs[SLOT[(end, 1)], z])
+                at = pl.ds(8 if end < 0 else rows + 4, 4)
+                for h in range(2):
+                    acc[depth + z, h, at, :] = acc[depth + z, h, at, :] + strip[pl.ds(4 * h, 4), :]
             for h in range(2):
                 total = acc[depth + z, h, pl.ds(8, rows), :] + (rz[0, z, h] + rz[1, z, h])
-                low = rs[SLOT[(-1, 0)], z, h] + (rs[SLOT[(-1, -1)], z, h] + rs[SLOT[(-1, 1)], z, h])
-                high = rs[SLOT[(1, 0)], z, h] + (rs[SLOT[(1, -1)], z, h] + rs[SLOT[(1, 1)], z, h])
-                total = jnp.concatenate(
-                    [total[:8] + low, total[8:rows - 8], total[rows - 8:] + high], axis=0)
                 est[depth + z, h, pl.ds(8, rows), :] = (
                     est[depth + z, h, pl.ds(8, rows), :] * (total * (1.0 / views)))
 
             @pl.when(step < ITERS - 1)
             def _():
-                each(SIDES, lambda side: est_copy(side, z).start())
+                send_estimate(z)
             return carry
 
         lax.fori_loop(0, depth, finish_plane, 0)
@@ -616,7 +629,11 @@
             pltpu.VMEM((views, depth, 2, frame, 128), F32),
             pltpu.VMEM((3 * depth, 2, frame, 128), F32),
             pltpu.VMEM((2, depth, 2, q, 128), F32),
-            pltpu.VMEM((8, depth, 2, 8, 128), F32),
+            pltpu.VMEM((8, depth, 8, 128), F32),
+            pltpu.VMEM((2, depth, 8, 128), F32),
+            pltpu.VMEM((8, depth, 8, 128), F32),
+            pltpu.VMEM((2, 3, depth, 8, 128), F32),
+            pltpu.VMEM((8, 128), F32),
             *[pltpu.VMEM((views, nx, nx), BF16)] * 4,
             pltpu.SemaphoreType.DMA((10,)),
             pltpu.SemaphoreType.DMA((10,)),

time: 135 us -> 133 us (0.985)
  Pallas kernels: 134 us -> 132 us
    pallas_call x1, Pallas kernels: 133 us -> 131 us  [whole(): pl.pallas_call(functools.partial(kernel, views, pencils), name='join_and_...]
where the time goes in v6:
time: 133 us
  Pallas kernels  132 us (99%)
    pallas_call x1, Pallas kernels, whole(): pl.pallas_call(functools.partial(kernel, views, pencils), name='join_and_...  131 us

profile of v6, /device:TPU:25, one launch (start us, length us, event | category | flops | bytes accessed | tf_op | source)
XLA Modules:
  0.0 132.6 jit_solution(2229580130080297641)
XLA Ops:
  0.6 131.2 %join_and_deconvolve.1 = (f32[4,64,256]{2,1,0:T(8,128)S(1)}, f32[4,64,256]{2,1,0:T(8,128)S(1)}) custom-call(f32[3,4,9]{2,1,0:T(4,128)} %bitcast.5, f32[4,256,256]{2,1,0:T(8,128)} %bitcast.3, f32[256,4,256]{2,1,0:T(4,128)} %bitcast.4, bf16[4,128,256]{2,1,0:T(8,128)(2,1)} %constant.20.clone.refs_0_, bf16[4,128,256]{2,1,0:T(8,128)(2,1)} %constant.21.clone.refs_1_, ...), custom_call_target="tpu_custom_call" | custom-call | tf_op jit(solution)/shard_map/join_and_deconvolve/pallas_call | solution.py:595
  131.8 0.8 store.1

commit v7 on v6

--- a/solution.py
+++ b/solution.py
@@ -462,7 +462,7 @@
             each(SIDES, lambda side: action(side, z))
             return carry
 
-        lax.fori_loop(0, planes, at_plane, 0)
+        lax.fori_loop(0, planes, at_plane, 0, unroll=True)
 
     def start_estimate(z, plane):
         out[z] = plane
@@ -558,7 +558,7 @@
                 send_estimate(z)
             return carry
 
-        lax.fori_loop(0, depth, finish_plane, 0)
+        lax.fori_loop(0, depth, finish_plane, 0, unroll=True)
         every_plane(lambda side, z: acc_copy(side, z).wait_send(), depth)
         return carry
 

time: 133 us -> 133 us (level)
  no operation moved by 1% of the time
where the time goes in v7:
time: 133 us
  Pallas kernels  132 us (99%)
    pallas_call x1, Pallas kernels, whole(): pl.pallas_call(functools.partial(kernel, views, pencils), name='join_and_...  131 us

profile of v7, /device:TPU:25, one launch (start us, length us, event | category | flops | bytes accessed | tf_op | source)
XLA Modules:
  0.0 132.6 jit_solution(228926332278668283)
XLA Ops:
  0.6 131.2 %join_and_deconvolve.1 = (f32[4,64,256]{2,1,0:T(8,128)S(1)}, f32[4,64,256]{2,1,0:T(8,128)S(1)}) custom-call(f32[3,4,9]{2,1,0:T(4,128)} %bitcast.5, f32[4,256,256]{2,1,0:T(8,128)} %bitcast.3, f32[256,4,256]{2,1,0:T(4,128)} %bitcast.4, bf16[4,128,256]{2,1,0:T(8,128)(2,1)} %constant.20.clone.refs_0_, bf16[4,128,256]{2,1,0:T(8,128)(2,1)} %constant.21.clone.refs_1_, ...), custom_call_target="tpu_custom_call" | custom-call | tf_op jit(solution)/shard_map/join_and_deconvolve/pallas_call | solution.py:595
  131.8 0.8 store.1
